TPU v7x, 64 devices: a 2x2x8 block of a 4x4x8 slice. The times are simulated.
64 devices in a mesh: dp: 4 (over x, y), ep: 16 (over z, core).
Axes of the slice: x: 2, y: 2, z: 8, core: 2. Of those that a mesh axis runs over, the one named last changes fastest.
The devices are a block of a 4x4x8 slice.
Arguments:
- tokens: bfloat16 [16384, 2048], P(('dp', 'ep')), parts along dimension 0
- expert_ids: int32 [16384, 6], P(('dp', 'ep')), parts along dimension 0
- gate_vals: float32 [16384, 6], P(('dp', 'ep')), parts along dimension 0
- slots: int32 [16384, 6], P(('dp', 'ep')), parts along dimension 0
- shared_w1: bfloat16 [2048, 2816], replicated
- shared_w3: bfloat16 [2048, 2816], replicated
- shared_w2: bfloat16 [2816, 2048], replicated
- shared_gate: bfloat16 [2048], replicated
- expert_w1: bfloat16 [64, 2048, 1408], P('ep')
- expert_w3: bfloat16 [64, 2048, 1408], P('ep')
- expert_w2: bfloat16 [64, 1408, 2048], P('ep')
Outputs:
- output: bfloat16 [16384, 2048], P(('dp', 'ep')), parts along dimension 0
There are 4 independent parts. A program takes and returns all parts, laid end to end along the dimension named above; an argument that names none is the same for every part.
All inputs are finite; a program needn't handle non-finite values.
Results may differ from a plain program's by a relative error of at most 0.00517458.
Values are sent between devices in bfloat16 or wider.
A program may use at most 768 MiB of HBM per device.

v0:
```python
import jax
import jax.numpy as jnp
from jax import lax
from jax.sharding import PartitionSpec as P


def solution(mesh):
    num_ep = mesh.shape['ep']
    row_spec = P(('dp', 'ep'), None)
    replicated = P()
    expert_spec = P('ep', None, None)

    def device_step(tokens, expert_ids, gate_vals, slots, shared_w1, shared_w3, shared_w2, shared_gate, expert_w1, expert_w3, expert_w2):
        tok_count, hidden = tokens.shape
        top_k = expert_ids.shape[1]
        local_experts = expert_w1.shape[0]
        num_experts = local_experts * num_ep
        capacity = 8 * ((2 * tok_count * top_k + 8 * num_experts - 1) // (8 * num_experts))
        buf_rows = num_experts * capacity
        kept_mask = slots >= 0
        slot_dest = jnp.where(kept_mask, expert_ids * capacity + slots, buf_rows)
        copy_tok = jnp.arange(tok_count * top_k, dtype=jnp.int32) // top_k
        row_owner = jnp.full((buf_rows + 1,), tok_count, jnp.int32).at[slot_dest.reshape(-1)].set(copy_tok)
        send_buf = jnp.take(tokens, row_owner[:buf_rows], axis=0, mode='fill', fill_value=0)
        recv_buf = lax.all_to_all(send_buf.reshape(num_ep, local_experts * capacity, hidden), 'ep', 0, 0, tiled=True)
        expert_in = recv_buf.reshape(num_ep, local_experts, capacity, hidden)
        act_a = jnp.einsum('secd,edf->secf', expert_in, expert_w1, preferred_element_type=jnp.float32)
        act_b = jnp.einsum('secd,edf->secf', expert_in, expert_w3, preferred_element_type=jnp.float32)
        hidden_act = (jax.nn.silu(act_a) * act_b).astype(jnp.bfloat16)
        expert_out = jnp.einsum('secf,efd->secd', hidden_act, expert_w2, preferred_element_type=jnp.float32).astype(jnp.bfloat16)
        back_buf = lax.all_to_all(expert_out.reshape(num_ep, local_experts * capacity, hidden), 'ep', 0, 0, tiled=True)
        picked = jnp.take(back_buf.reshape(buf_rows, hidden), slot_dest, axis=0, mode='fill', fill_value=0)
        weights = jnp.where(kept_mask, gate_vals, 0.0)[:, :, None]
        routed = jnp.sum(weights * picked, axis=1)
        gate_logit = jnp.dot(tokens, shared_gate, preferred_element_type=jnp.float32)
        shared_a = jnp.dot(tokens, shared_w1, preferred_element_type=jnp.float32)
        shared_b = jnp.dot(tokens, shared_w3, preferred_element_type=jnp.float32)
        shared_h = (jax.nn.silu(shared_a) * shared_b).astype(jnp.bfloat16)
        shared_out = jnp.dot(shared_h, shared_w2, preferred_element_type=jnp.float32)
        total = tokens.astype(jnp.float32) + jax.nn.sigmoid(gate_logit)[:, None] * shared_out + routed
        return total.astype(jnp.bfloat16)

    return jax.shard_map(device_step, mesh=mesh, in_specs=(row_spec, row_spec, row_spec, row_spec, replicated, replicated, replicated, replicated, expert_spec, expert_spec, expert_spec), out_specs=row_spec, check_vma=False)
```

profile of v0, /device:TPU:21, one launch (start us, length us, event | category | flops | bytes accessed | tf_op | source)
XLA Modules:
  0.0 771.1 jit_solution(3046420441432136661)
XLA Ops:
  0.0 1.3 compare_and_fusion.1
  1.3 0.0 copy-start.1
  1.3 0.1 copy.16
  1.4 0.1 reshape.60
  1.6 6.2 scatter_custom_fusion
  7.8 0.1 slice.6
  7.9 25.2 %gather_fusion = bf16[3072,2048]{1,0:T(8,128)(2,1)} fusion(bf16[256,2048]{1,0:T(8,128)(2,1)} %param.11, s32[3072]{0:T(1024)S(1)} %get-tuple-element.8), kind=kCustom, calls=%fused_computation | custom fusion | bytes 25178112 | tf_op jit(solution)/shard_map/jit(_take)/gather | solution.py:24
  33.1 0.0 copy-done.1
  33.1 6.4 broadcast_select_fusion
  39.5 286.5 %all_to_all.10 = bf16[16,192,2048]{2,1,0:T(8,128)(2,1)} all-to-all(bf16[16,192,2048]{2,1,0:T(8,128)(2,1)S(1)} %broadcast_select_fusion), channel_id=1, replica_groups=mesh['dp'=4,'ep'=16] {'ep'}, dimensions={0} | all-to-all | bytes 25165824 | tf_op jit(solution)/shard_map/all_to_all | solution.py:25
  326.0 29.2 %fusion.2 = f32[4,16,48,1408]{3,2,1,0:T(8,128)} fusion(bf16[4,2048,1408]{2,1,0:T(8,128)(2,1)} %param.20, bf16[16,4,48,2048]{3,2,1,0:T(8,128)(2,1)} %bitcast.53), kind=kOutput, calls=%fused_computation.5 | convolution fusion | flops 17716740096 | bytes 52953088 | tf_op jit(solution)/shard_map/secd,edf->secf/dot_general | solution.py:28
  355.2 32.3 %fusion.6 = bf16[16,4,48,1408]{3,2,0,1:T(8,128)(2,1)} fusion(f32[4,16,48,1408]{3,2,1,0:T(8,128)} %fusion.2, bf16[4,2048,1408]{2,1,0:T(8,128)(2,1)} %param.19, bf16[16,4,48,2048]{3,2,1,0:T(8,128)(2,1)} %bitcast.54), kind=kOutput, calls=%fused_computation.10 | convolution fusion | flops 17742692352 | bytes 61603840 | tf_op jit(solution)/shard_map/secd,edf->secf/dot_general | solution.py:27
  387.5 27.0 %convert_bitcast_fusion = bf16[16,4,48,2048]{3,2,0,1:T(8,128)(2,1)} fusion(bf16[16,4,48,1408]{3,2,0,1:T(8,128)(2,1)} %fusion.6, bf16[4,1408,2048]{2,1,0:T(8,128)(2,1)} %param.21), kind=kOutput, calls=%fused_computation.17 | convolution fusion | flops 17723031552 | bytes 44302336 | tf_op jit(solution)/shard_map/secf,efd->secd/dot_general | solution.py:30
  414.4 10.7 %copy.18 = bf16[16,4,48,2048]{3,2,1,0:T(8,128)(2,1)} copy(bf16[16,4,48,2048]{3,2,0,1:T(8,128)(2,1)} %convert_bitcast_fusion) | data formatting | bytes 25165824 | tf_op jit(solution)/shard_map/convert_element_type | solution.py:30
  425.2 0.0 copy-start.2
  425.2 0.0 copy-start.5
  425.2 0.0 copy-start.3
  425.2 0.0 copy-start.4
  425.2 0.0 copy-start.6
  425.2 0.0 copy-start
  425.2 5.2 all-to-all-start.1
  430.4 0.0 copy-done.2
  430.4 0.1 copy.19
  430.6 0.1 reshape.74
  430.7 0.0 copy-done.5
  430.7 0.2 copy.15
  430.9 0.0 copy-done.3
  430.9 0.0 copy-done.4
  430.9 0.1 copy.14
  431.1 0.0 copy-done.6
  431.1 0.0 copy-done
  431.1 0.4 fusion.29
  431.5 9.1 %fusion.30 = f32[256,2816]{1,0:T(8,128)} fusion(bf16[256,2048]{1,0:T(8,128)(2,1)S(1)} %copy-done, bf16[2048,2816]{1,0:T(8,128)(2,1)} %param.15), kind=kOutput, calls=%fused_computation.52 | convolution fusion | flops 2952790016 | bytes 15466496 | tf_op jit(solution)/shard_map/dot_general | solution.py:36
  440.6 274.3 %all-to-all-done.1 = bf16[16,192,2048]{2,1,0:T(8,128)(2,1)} async-done(((bf16[16,192,2048]{2,1,0:T(8,128)(2,1)}), bf16[16,192,2048]{2,1,0:T(8,128)(2,1)}, u32[]{:S(2)}, u32[]{:S(2)}) %all-to-all-start.1) | async-done | bytes 12582944 | tf_op jit(solution)/shard_map/all_to_all | solution.py:31
  714.9 18.9 %gather_fusion.1 = bf16[1536,2048]{1,0:T(8,128)(2,1)} fusion(bf16[3072,2048]{1,0:T(8,128)(2,1)} %bitcast.13, s32[2048]{0:T(1024)S(1)} %pad_clamp_fusion), kind=kCustom, calls=%fused_computation.1 | custom fusion | bytes 12589056 | tf_op jit(solution)/shard_map/jit(_take)/gather | solution.py:32
  733.9 11.0 %reshape.73 = bf16[256,6,2048]{2,1,0:T(8,128)(2,1)} reshape(bf16[1536,2048]{1,0:T(8,128)(2,1)} %gather_fusion.1) | data formatting | bytes 12582912 | tf_op jit(solution)/shard_map/jit(_take)/gather | solution.py:32
  744.8 10.6 %multiply_reduce_fusion = f32[256,2048]{1,0:T(8,128)S(1)} fusion(bf16[256,6,2048]{2,1,0:T(8,128)(2,1)} %reshape.73, f32[256,6]{1,0:T(8,128)S(1)} %copy.14, pred[256,6]{1,0:T(8,128)(4,1)S(1)} %copy.15), kind=kLoop, calls=%fused_computation.16 | loop fusion | flops 12058624 | bytes 8396288 | tf_op jit(solution)/shard_map/reduce_sum | solution.py:34
  755.4 15.6 %fusion.19 = bf16[256,2048]{1,0:T(8,128)(2,1)} fusion(f32[256,2048]{1,0:T(8,128)S(1)} %multiply_reduce_fusion, bf16[2816,2048]{1,0:T(8,128)(2,1)} %param.17, bf16[256,2048]{1,0:T(8,128)(2,1)S(1)} %copy-done, f32[256]{0:T(256)S(1)} %add_divide_fusion, bf16[2048,2816]{1,0:T(8,128)(2,1)} %param.16, f32[256,2816]{1,0:T(8,128)} %fusion.30), kind=kOutput, calls=%fused_computation.26 | convolution fusion | flops 5912526848 | bytes 30147584 | tf_op jit(solution)/shard_map/dot_general | solution.py:39
  (9 shorter events, 0.1 us)
Async XLA Ops:
  1.3 31.8 %copy-start.1 = (s32[256,6]{0,1:T(8,128)}, s32[256,6]{0,1:T(8,128)S(1)}, u32[]{:S(2)}) copy-start(s32[256,6]{0,1:T(8,128)S(1)} %get-tuple-element.6) | copy-start | bytes 18436
  425.2 5.2 copy-start.2
  425.2 5.5 copy-start.5
  425.2 5.7 copy-start.3
  425.2 5.7 copy-start.4
  425.2 5.9 copy-start.6
  425.2 5.9 copy-start
  425.2 289.7 %all-to-all-start.1 = ((bf16[16,192,2048]{2,1,0:T(8,128)(2,1)}), bf16[16,192,2048]{2,1,0:T(8,128)(2,1)}, u32[]{:S(2)}, u32[]{:S(2)}) async-start(bf16[16,192,2048]{2,1,0:T(8,128)(2,1)} %bitcast.51), calls=%async_computation.1 | async-start | bytes 25165824 | tf_op jit(solution)/shard_map/all_to_all | solution.py:31
where the time goes:
time: 772 us; the launch traced here: 771 us
  blocking collectives  287 us (37%)
  waiting for transfers between devices  274 us (35%)
  matrix products  114 us (15%)
  local copies, waits for them, and re-layouts  73 us (9%)
  other arithmetic  18.3 us (2%)
    all_to_all x1, blocking collectives, device_step(): lax.all_to_all(send_buf.reshape(num_ep, local_experts * capacity, hidden)...  287 us
    all_to_all x1, waiting for transfers between devices, device_step(): lax.all_to_all(expert_out.reshape(num_ep, local_experts * capacity, hidde...  274 us
    dot_general x1, matrix products, device_step(): jnp.einsum('secd,edf->secf', expert_in, expert_w1, preferred_element_type...  32.3 us
    gather x2, local copies, waits for them, and re-layouts, device_step(): jnp.take(back_buf.reshape(buf_rows, hidden), slot_dest, axis=0, mode='fil...  29.9 us
    dot_general x1, matrix products, device_step(): jnp.einsum('secd,edf->secf', expert_in, expert_w3, preferred_element_type...  29.2 us
    dot_general x1, matrix products, device_step(): jnp.einsum('secf,efd->secd', hidden_act, expert_w2, preferred_element_typ...  27 us
    gather x1, local copies, waits for them, and re-layouts, device_step(): jnp.take(tokens, row_owner[:buf_rows], axis=0, mode='fill', fill_value=0)  25.2 us
    dot_general x1, matrix products, device_step(): jnp.dot(shared_h, shared_w2, preferred_element_type=jnp.float32)  15.6 us
  transfers between devices with their start and end apart: 1, of which 1 were waited for; matrix products, arithmetic and copies ran while one was open for 1% of the time, Pallas kernels for 0%

commit v1 on v0

v1 whole, which is shorter than its diff:
```python
import jax
import jax.numpy as jnp
from jax import lax
from jax.sharding import PartitionSpec as P


def solution(mesh):
    num_ep = mesh.shape['ep']
    nz = num_ep // 2
    half = nz // 2
    row_spec = P(('dp', 'ep'), None)
    replicated = P()
    expert_spec = P('ep', None, None)
    plus = [(i, (i + 2) % num_ep) for i in range(num_ep)]
    minus = [(i, (i - 2) % num_ep) for i in range(num_ep)]
    swap = [(i, i ^ 1) for i in range(num_ep)]

    def send(x, perm):
        return lax.ppermute(x, 'ep', perm)

    def after(x, dep):
        return lax.optimization_barrier((x, dep))[0]

    def device_step(tokens, expert_ids, gate_vals, slots, shared_w1, shared_w3, shared_w2, shared_gate, expert_w1, expert_w3, expert_w2):
        tok_count, hidden = tokens.shape
        top_k = expert_ids.shape[1]
        local_experts = expert_w1.shape[0]
        num_experts = local_experts * num_ep
        capacity = 8 * ((2 * tok_count * top_k + 8 * num_experts - 1) // (8 * num_experts))
        core_rows = local_experts * capacity
        chip_rows = 2 * core_rows
        ep = lax.axis_index('ep')
        z, core = ep // 2, ep % 2
        half_tok = tok_count // 2

        code = jnp.where(slots >= 0, expert_ids * capacity + slots, -1).astype(jnp.float32)
        meta = jnp.concatenate([code.T, gate_vals.T, jnp.zeros((16 - 2 * top_k, tok_count), jnp.float32)], axis=0)

        fwd_tok, fwd_meta = [tokens], [meta]
        bwd_tok, bwd_meta = [tokens], [meta]
        for hop in range(1, half):
            fwd_meta.append(send(fwd_meta[-1], plus))
            bwd_meta.append(send(bwd_meta[-1], minus))
            fwd_tok.append(send(fwd_tok[-1], plus))
            bwd_tok.append(send(bwd_tok[-1], minus))
        far_meta = send(fwd_meta[-1], plus)
        far_tok = jnp.concatenate([send(fwd_tok[-1][:half_tok], plus), send(bwd_tok[-1][half_tok:], minus)], axis=0)

        def relative(m):
            c = m[:top_k].astype(jnp.int32)
            rel = c - z * chip_rows
            inside = (c >= 0) & (rel >= 0) & (rel < chip_rows)
            rel = (rel - core * core_rows) % chip_rows
            return jnp.where(inside, rel, -1)

        def gather_rows(blocks, metas):
            rel = jnp.stack([relative(m) for m in metas])
            x = jnp.stack(blocks)
            pos = lax.broadcasted_iota(jnp.int32, (len(blocks), chip_rows, tok_count), 1)
            hit = jnp.zeros(pos.shape, jnp.bool_)
            for k in range(top_k):
                hit = hit | (pos == rel[:, k][:, None, :])
            sel = hit.astype(jnp.bfloat16)
            return jnp.einsum('nst,ntd->nsd', sel, x, preferred_element_type=jnp.float32).astype(jnp.bfloat16)

        def exchange(rows):
            n = rows.shape[0]
            other = send(rows[:, core_rows:], swap)
            both = jnp.concatenate([rows[:, :core_rows], other], axis=0)
            return both.reshape(2 * n, local_experts, capacity, hidden)

        def ffn(rows):
            act_a = jnp.einsum('secd,edf->secf', rows, expert_w1, preferred_element_type=jnp.float32)
            act_b = jnp.einsum('secd,edf->secf', rows, expert_w3, preferred_element_type=jnp.float32)
            h = (jax.nn.silu(act_a) * act_b).astype(jnp.bfloat16)
            return jnp.einsum('secf,efd->secd', h, expert_w2, preferred_element_type=jnp.float32).astype(jnp.bfloat16)

        def give_back(res):
            n = res.shape[0] // 2
            res = res.reshape(2 * n, core_rows, hidden)
            other = send(res[n:], swap)
            return jnp.concatenate([res[:n], other], axis=1)

        def combine(res, metas):
            rel = jnp.stack([relative(m).T for m in metas])
            gate = jnp.stack([m[top_k:2 * top_k].T for m in metas])
            pos = lax.broadcasted_iota(jnp.int32, (len(metas), tok_count, chip_rows), 2)
            w = jnp.zeros(pos.shape, jnp.float32)
            for k in range(top_k):
                w = jnp.where(pos == rel[:, :, k][:, :, None], gate[:, :, k][:, :, None], w)
            hi = lax.reduce_precision(w, 8, 7)
            rest = w - hi
            mid = lax.reduce_precision(rest, 8, 7)
            low = rest - mid
            w3 = jnp.concatenate([hi.astype(jnp.bfloat16), mid.astype(jnp.bfloat16), low.astype(jnp.bfloat16)], axis=2)
            res3 = jnp.concatenate([res, res, res], axis=1)
            return jnp.einsum('nts,nsd->ntd', w3, res3, preferred_element_type=jnp.float32)

        gate_logit = jnp.dot(tokens, shared_gate, preferred_element_type=jnp.float32)
        shared_a = jnp.dot(tokens, shared_w1, preferred_element_type=jnp.float32)
        shared_b = jnp.dot(tokens, shared_w3, preferred_element_type=jnp.float32)
        shared_h = (jax.nn.silu(shared_a) * shared_b).astype(jnp.bfloat16)
        shared_out = jnp.dot(shared_h, shared_w2, preferred_element_type=jnp.float32)
        base = tokens.astype(jnp.float32) + jax.nn.sigmoid(gate_logit)[:, None] * shared_out

        part = {}
        order = [0, 1, half] + list(range(half - 1, 1, -1))
        dep = base
        for d in order:
            if d == 0:
                blocks, metas = [tokens], [meta]
            elif d == half:
                blocks, metas = [far_tok], [far_meta]
            else:
                blocks, metas = [bwd_tok[d], fwd_tok[d]], [bwd_meta[d], fwd_meta[d]]
            rows = exchange(gather_rows(blocks, metas))
            rows = after(rows, dep)
            res = ffn(rows)
            dep = res
            part[d] = combine(give_back(res), metas)

        far = part[half][0]
        got_p = send(far[:half_tok], plus)
        got_m = send(far[half_tok:], minus)
        for d in range(half - 1, 0, -1):
            mine_p, mine_m = part[d][0], part[d][1]
            if d == half - 1:
                mine_p = jnp.concatenate([mine_p[:half_tok] + got_p, mine_p[half_tok:]], axis=0)
                mine_m = jnp.concatenate([mine_m[:half_tok], mine_m[half_tok:] + got_m], axis=0)
            else:
                mine_p = mine_p + got_p
                mine_m = mine_m + got_m
            got_p = send(mine_p, plus)
            got_m = send(mine_m, minus)
        total = base + part[0][0] + got_p + got_m
        return total.astype(jnp.bfloat16)

    return jax.shard_map(device_step, mesh=mesh, in_specs=(row_spec, row_spec, row_spec, row_spec, replicated, replicated, replicated, replicated, expert_spec, expert_spec, expert_spec), out_specs=row_spec, check_vma=False)
```

time: 772 us -> 491 us (0.64)
  the two profiles are of different devices: /device:TPU:21 before, /device:TPU:28 now
where the time goes in v1:
time: 491 us; the launch traced here: 482 us
  matrix products  229 us (47%)
  waiting for transfers between devices  153 us (31%)
  starting transfers between devices  45.2 us (9%)
  local copies, waits for them, and re-layouts  34.1 us (7%)
  other arithmetic  18.2 us (4%)
    ppermute x33, waiting for transfers between devices, send(): return lax.ppermute(x, 'ep', perm)  153 us
    dot_general x5, matrix products, ffn(): jnp.einsum('secd,edf->secf', rows, expert_w1, preferred_element_type=jnp....  60.7 us
    dot_general x5, matrix products, ffn(): jnp.einsum('secd,edf->secf', rows, expert_w3, preferred_element_type=jnp....  59.8 us
    dot_general x5, matrix products, ffn(): jnp.einsum('secf,efd->secd', h, expert_w2, preferred_element_type=jnp.flo...  54.1 us
    ppermute x33, starting transfers between devices, send(): return lax.ppermute(x, 'ep', perm)  45.2 us
    unnamed x121, local copies, waits for them, and re-layouts  21.5 us
    dot_general x5, matrix products, combine(): jnp.einsum('nts,nsd->ntd', w3, res3, preferred_element_type=jnp.float32)  18.6 us
    dot_general x1, matrix products, device_step(): jnp.dot(shared_h, shared_w2, preferred_element_type=jnp.float32)  15.9 us
  transfers between devices with their start and end apart: 33, of which 12 were waited for; matrix products, arithmetic and copies ran while one was open for 55% of the time, Pallas kernels for 0%

profile of v1, /device:TPU:28, one launch (start us, length us, event | category | flops | bytes accessed | tf_op | source)
XLA Modules:
  0.0 481.9 jit_solution(9876394668884037417)
XLA Ops:
  2.1 5.3 %collective-permute-start.4 = (bf16[256,2048]{1,0:T(8,128)(2,1)}, bf16[256,2048]{1,0:T(8,128)(2,1)}, u32[]{:S(2)}, u32[]{:S(2)}) collective-permute-start(bf16[256,2048]{1,0:T(8,128)(2,1)} %param.11), channel_id=1, source_target_pairs={{0,14},{1,15},{2,0},{3,1},{4,2},{5,3},{6,4},{7,5},{8,6},{9,7},{10,... | collective-permute-start | bytes 3145736 | tf_op jit(solution)/shard_map/ppermute | solution.py:19
  9.0 3.2 collective-permute-start.2
  14.9 9.0 %fusion.300 = f32[256,2816]{1,0:T(8,128)} fusion(bf16[256,2048]{1,0:T(8,128)(2,1)S(1)} %copy-done.3, bf16[2048,2816]{1,0:T(8,128)(2,1)} %param.15), kind=kOutput, calls=%fused_computation.541 | convolution fusion | flops 2952790016 | bytes 15466496 | tf_op jit(solution)/shard_map/dot_general | solution.py:100
  23.9 15.9 %fusion.107 = f32[256,2048]{1,0:T(8,128)} fusion(bf16[2816,2048]{1,0:T(8,128)(2,1)} %param.17, bf16[256,2048]{1,0:T(8,128)(2,1)S(1)} %copy-done.3, f32[256]{0:T(256)S(1)} %add_divide_fusion, bf16[2048,2816]{1,0:T(8,128)(2,1)} %param.16, f32[256,2816]{1,0:T(8,128)} %fusion.300), kind=kOutput, calls=%fused_computation.88 | convolution fusion | flops 5911478272 | bytes 29099008 | tf_op jit(solution)/shard_map/dot_general | solution.py:103
  40.7 2.3 reduce-precision_convert_fusion.5
  43.0 3.2 collective-permute-start.8
  48.2 2.3 reduce-precision_convert_fusion.3
  50.5 3.5 collective-permute-start.13
  55.7 2.4 reduce-precision_convert_fusion.1
  58.1 2.5 collective-permute-start.18
  60.6 2.7 collective-permute-done.18
  64.9 9.5 %fusion.62 = f32[2,4,48,1408]{3,2,0,1:T(8,128)S(1)} fusion(bf16[4,2048,1408]{2,1,0:T(8,128)(2,1)} %param.19, bf16[2,4,48,2048]{3,2,1,0:T(8,128)(2,1)S(1)} %bitcast.471), kind=kOutput, calls=%fused_computation.66 | convolution fusion | flops 2214592512 | bytes 26804224 | tf_op jit(solution)/shard_map/secd,edf->secf/dot_general | solution.py:73
  74.4 11.5 %fusion.98 = bf16[2,4,48,1408]{3,2,0,1:T(8,128)(2,1)S(1)} fusion(bf16[4,2048,1408]{2,1,0:T(8,128)(2,1)} %param.20, f32[2,4,48,1408]{3,2,0,1:T(8,128)S(1)} %fusion.62, bf16[2,4,48,2048]{3,2,1,0:T(8,128)(2,1)S(1)} %bitcast.472), kind=kOutput, calls=%fused_computation.78 | convolution fusion | flops 2217836544 | bytes 27885568 | tf_op jit(solution)/shard_map/secd,edf->secf/dot_general | solution.py:74
  85.9 2.8 convolution_convert_fusion.2
  92.5 11.5 %fusion.120 = bf16[2,4,48,2048]{3,2,0,1:T(8,128)(2,1)S(1)} fusion(bf16[2,4,48,1408]{3,2,0,1:T(8,128)(2,1)S(1)} %fusion.98, bf16[4,1408,2048]{2,1,0:T(8,128)(2,1)} %param.21), kind=kOutput, calls=%fused_computation.93 | convolution fusion | flops 2215378944 | bytes 25722880 | tf_op jit(solution)/shard_map/secf,efd->secd/dot_general | solution.py:76
  105.7 10.2 %collective-permute-done.11 = bf16[256,2048]{1,0:T(8,128)(2,1)} collective-permute-done((bf16[256,2048]{1,0:T(8,128)(2,1)}, bf16[256,2048]{1,0:T(8,128)(2,1)}, u32[]{:S(2)}, u32[]{:S(2)}) %collective-permute-start.11) | collective-permute-done | bytes 1048608 | tf_op jit(solution)/shard_map/ppermute | solution.py:19
  115.9 2.8 convolution_convert_fusion.1
  123.6 12.3 %fusion.16 = f32[4,4,48,1408]{3,2,1,0:T(8,128)} fusion(bf16[4,2048,1408]{2,1,0:T(8,128)(2,1)} %param.20, bf16[4,4,48,2048]{3,2,1,0:T(8,128)(2,1)S(1)} %bitcast.492), kind=kOutput, calls=%fused_computation.16 | convolution fusion | flops 4429185024 | bytes 30539776 | tf_op jit(solution)/shard_map/secd,edf->secf/dot_general | solution.py:74
  136.0 11.6 %fusion.42 = bf16[4,4,48,1408]{3,2,0,1:T(8,128)(2,1)S(1)} fusion(f32[4,4,48,1408]{3,2,1,0:T(8,128)} %fusion.16, bf16[4,2048,1408]{2,1,0:T(8,128)(2,1)} %param.19, bf16[4,4,48,2048]{3,2,1,0:T(8,128)(2,1)S(1)} %bitcast.493), kind=kOutput, calls=%fused_computation.49 | convolution fusion | flops 4435673088 | bytes 32702464 | tf_op jit(solution)/shard_map/secd,edf->secf/dot_general | solution.py:73
  147.6 10.4 %fusion.86 = bf16[4,4,48,2048]{3,2,0,1:T(8,128)(2,1)S(1)} fusion(bf16[4,4,48,1408]{3,2,0,1:T(8,128)(2,1)S(1)} %fusion.42, bf16[4,1408,2048]{2,1,0:T(8,128)(2,1)} %param.21), kind=kOutput, calls=%fused_computation.74 | convolution fusion | flops 4430757888 | bytes 28377088 | tf_op jit(solution)/shard_map/secf,efd->secd/dot_general | solution.py:76
  164.7 2.5 convolution_convert_fusion
  167.2 8.2 %collective-permute-done.20 = bf16[128,2048]{1,0:T(8,128)(2,1)S(1)} collective-permute-done((bf16[128,2048]{1,0:T(8,128)(2,1)S(1)}, bf16[128,2048]{1,0:T(8,128)(2,1)S(1)}, u32[]{:S(2)}, u32[]{:S(2)}) %collective-permute-start.20) | collective-permute-done | bytes 524320 | tf_op jit(solution)/shard_map/ppermute | solution.py:19
  175.5 3.0 collective-permute-done.19
  180.5 3.3 pad_maximum_fusion.1
  184.0 9.5 %fusion.65 = f32[2,4,48,1408]{3,2,0,1:T(8,128)S(1)} fusion(bf16[4,2048,1408]{2,1,0:T(8,128)(2,1)} %param.19, bf16[2,4,48,2048]{3,2,1,0:T(8,128)(2,1)S(1)} %bitcast.473), kind=kOutput, calls=%fused_computation.67 | convolution fusion | flops 2214592512 | bytes 26804224 | tf_op jit(solution)/shard_map/secd,edf->secf/dot_general | solution.py:73
  193.5 11.5 %fusion.95 = bf16[2,4,48,1408]{3,2,0,1:T(8,128)(2,1)S(1)} fusion(bf16[4,2048,1408]{2,1,0:T(8,128)(2,1)} %param.20, f32[2,4,48,1408]{3,2,0,1:T(8,128)S(1)} %fusion.65, bf16[2,4,48,2048]{3,2,1,0:T(8,128)(2,1)S(1)} %bitcast.474), kind=kOutput, calls=%fused_computation.77 | convolution fusion | flops 2217836544 | bytes 27885568 | tf_op jit(solution)/shard_map/secd,edf->secf/dot_general | solution.py:74
  205.0 11.6 %fusion.117 = bf16[2,4,48,2048]{3,2,0,1:T(8,128)(2,1)S(1)} fusion(bf16[2,4,48,1408]{3,2,0,1:T(8,128)(2,1)S(1)} %fusion.95, bf16[4,1408,2048]{2,1,0:T(8,128)(2,1)} %param.21), kind=kOutput, calls=%fused_computation.92 | convolution fusion | flops 2215378944 | bytes 25722880 | tf_op jit(solution)/shard_map/secf,efd->secd/dot_general | solution.py:76
  219.9 12.3 %fusion.12 = f32[4,4,48,1408]{3,2,1,0:T(8,128)} fusion(bf16[4,2048,1408]{2,1,0:T(8,128)(2,1)} %param.20, bf16[4,4,48,2048]{3,2,1,0:T(8,128)(2,1)S(1)} %bitcast.494), kind=kOutput, calls=%fused_computation.12 | convolution fusion | flops 4429185024 | bytes 30539776 | tf_op jit(solution)/shard_map/secd,edf->secf/dot_general | solution.py:74
  232.1 15.0 %fusion.38 = bf16[4,4,48,1408]{3,2,0,1:T(8,128)(2,1)S(1)} fusion(f32[4,4,48,1408]{3,2,1,0:T(8,128)} %fusion.12, bf16[4,2048,1408]{2,1,0:T(8,128)(2,1)} %param.19, bf16[4,4,48,2048]{3,2,1,0:T(8,128)(2,1)} %bitcast.495), kind=kOutput, calls=%fused_computation.42 | convolution fusion | flops 4435673088 | bytes 32702464 | tf_op jit(solution)/shard_map/secd,edf->secf/dot_general | solution.py:73
  247.2 10.4 %fusion.83 = bf16[4,4,48,2048]{3,2,0,1:T(8,128)(2,1)S(1)} fusion(bf16[4,4,48,1408]{3,2,0,1:T(8,128)(2,1)S(1)} %fusion.38, bf16[4,1408,2048]{2,1,0:T(8,128)(2,1)} %param.21), kind=kOutput, calls=%fused_computation.73 | convolution fusion | flops 4430757888 | bytes 28377088 | tf_op jit(solution)/shard_map/secf,efd->secd/dot_general | solution.py:76
  260.2 12.3 %fusion.10 = f32[4,4,48,1408]{3,2,1,0:T(8,128)} fusion(bf16[4,2048,1408]{2,1,0:T(8,128)(2,1)} %param.20, bf16[4,4,48,2048]{3,2,1,0:T(8,128)(2,1)S(1)} %bitcast.491), kind=kOutput, calls=%fused_computation.10 | convolution fusion | flops 4429185024 | bytes 30539776 | tf_op jit(solution)/shard_map/secd,edf->secf/dot_general | solution.py:74
  272.5 15.0 %fusion.34 = bf16[4,4,48,1408]{3,2,0,1:T(8,128)(2,1)S(1)} fusion(f32[4,4,48,1408]{3,2,1,0:T(8,128)} %fusion.10, bf16[4,2048,1408]{2,1,0:T(8,128)(2,1)} %param.19, bf16[4,4,48,2048]{3,2,1,0:T(8,128)(2,1)} %bitcast.490), kind=kOutput, calls=%fused_computation.35 | convolution fusion | flops 4435673088 | bytes 32702464 | tf_op jit(solution)/shard_map/secd,edf->secf/dot_general | solution.py:73
  287.5 10.3 %fusion.80 = bf16[4,4,48,2048]{3,2,0,1:T(8,128)(2,1)S(1)} fusion(bf16[4,4,48,1408]{3,2,0,1:T(8,128)(2,1)S(1)} %fusion.34, bf16[4,1408,2048]{2,1,0:T(8,128)(2,1)} %param.21), kind=kOutput, calls=%fused_computation.72 | convolution fusion | flops 4430757888 | bytes 28377088 | tf_op jit(solution)/shard_map/secf,efd->secd/dot_general | solution.py:76
  304.3 3.4 collective-permute-start.29
  308.2 3.7 copy-done.17
  311.9 5.7 %fusion.157 = f32[2,256,2048]{2,1,0:T(8,128)S(1)} fusion(bf16[2,1152,2048]{2,1,0:T(8,128)(2,1)} %copy-done.17, bf16[2,256,384]{2,1,0:T(8,128)(2,1)S(1)} %copy-done.14, bf16[2,256,384]{2,1,0:T(8,128)(2,1)S(1)} %copy-done.15, bf16[2,256,384]{2,1,0:T(8,128)(2,1)S(1)} %copy-done.13), kind=kOutput, calls=%fused_computation.134 | convolution fusion | flops 2419458048 | bytes 14811136 | tf_op jit(solution)/shard_map/nts,nsd->ntd/dot_general | solution.py:97
  317.8 13.2 %collective-permute-done.25 = f32[128,2048]{1,0:T(8,128)S(1)} collective-permute-done((f32[128,2048]{1,0:T(8,128)S(1)}, f32[128,2048]{1,0:T(8,128)S(1)}, u32[]{:S(2)}, u32[]{:S(2)}) %collective-permute-start.25) | collective-permute-done | bytes 1048608 | tf_op jit(solution)/shard_map/ppermute | solution.py:19
  331.7 3.3 collective-permute-start.30
  335.9 3.5 copy-done.16
  339.5 5.7 %fusion.151 = f32[2,256,2048]{2,1,0:T(8,128)S(1)} fusion(bf16[2,1152,2048]{2,1,0:T(8,128)(2,1)} %copy-done.16, bf16[2,256,384]{2,1,0:T(8,128)(2,1)S(1)} %copy-done.11, bf16[2,256,384]{2,1,0:T(8,128)(2,1)S(1)} %copy-done.12, bf16[2,256,384]{2,1,0:T(8,128)(2,1)S(1)} %copy-done.10), kind=kOutput, calls=%fused_computation.128 | convolution fusion | flops 2419458048 | bytes 14811136 | tf_op jit(solution)/shard_map/nts,nsd->ntd/dot_general | solution.py:97
  345.2 34.7 %collective-permute-done.26 = f32[256,2048]{1,0:T(8,128)S(1)} collective-permute-done((f32[256,2048]{1,0:T(8,128)S(1)}, f32[256,2048]{1,0:T(8,128)S(1)}, u32[]{:S(2)}, u32[]{:S(2)}) %collective-permute-start.26) | collective-permute-done | bytes 2097184 | tf_op jit(solution)/shard_map/ppermute | solution.py:19
  381.0 2.2 collective-permute-start.27
  389.4 2.9 fusion.145
  392.3 36.4 %collective-permute-done.27 = f32[256,2048]{1,0:T(8,128)S(1)} collective-permute-done((f32[256,2048]{1,0:T(8,128)S(1)}, f32[256,2048]{1,0:T(8,128)S(1)}, u32[]{:S(2)}, u32[]{:S(2)}) %collective-permute-start.27) | collective-permute-done | bytes 2097184 | tf_op jit(solution)/shard_map/ppermute | solution.py:19
  430.1 2.8 collective-permute-start.32
  437.4 38.1 %collective-permute-done.32 = f32[256,2048]{1,0:T(8,128)S(1)} collective-permute-done((f32[256,2048]{1,0:T(8,128)S(1)}, f32[256,2048]{1,0:T(8,128)S(1)}, u32[]{:S(2)}, u32[]{:S(2)}) %collective-permute-start.32) | collective-permute-done | bytes 2097184 | tf_op jit(solution)/shard_map/ppermute | solution.py:19
  475.5 3.4 collective-permute-done.28
  479.0 2.8 fusion.125
  (245 shorter events, 58.7 us)
Async XLA Ops:
  0.0 14.5 %copy-start.3 = (bf16[256,2048]{1,0:T(8,128)(2,1)S(1)}, bf16[256,2048]{1,0:T(8,128)(2,1)}, u32[]{:S(2)}) copy-start(bf16[256,2048]{1,0:T(8,128)(2,1)} %param.11) | copy-start | bytes 3145732
  0.0 14.4 %copy-start.25 = (bf16[2048]{0:T(1024)(128)(2,1)S(1)}, bf16[2048]{0:T(1024)(128)(2,1)}, u32[]{:S(2)}) copy-start(bf16[2048]{0:T(1024)(128)(2,1)} %param.18) | copy-start | bytes 12292
  0.0 85.9 %collective-permute-start.5 = (bf16[256,2048]{1,0:T(8,128)(2,1)}, bf16[256,2048]{1,0:T(8,128)(2,1)}, u32[]{:S(2)}, u32[]{:S(2)}) collective-permute-start(bf16[256,2048]{1,0:T(8,128)(2,1)} %param.11), channel_id=1, source_target_pairs={{0,2},{1,3},{2,4},{3,5},{4,6},{5,7},{6,8},{7,9},{8,10},{9,11},{10,... | collective-permute-start | bytes 3145736 | tf_op jit(solution)/shard_map/ppermute | solution.py:19
  2.1 83.8 %collective-permute-start.4 = (bf16[256,2048]{1,0:T(8,128)(2,1)}, bf16[256,2048]{1,0:T(8,128)(2,1)}, u32[]{:S(2)}, u32[]{:S(2)}) collective-permute-start(bf16[256,2048]{1,0:T(8,128)(2,1)} %param.11), channel_id=1, source_target_pairs={{0,14},{1,15},{2,0},{3,1},{4,2},{5,3},{6,4},{7,5},{8,6},{9,7},{10,... | collective-permute-start | bytes 3145736 | tf_op jit(solution)/shard_map/ppermute | solution.py:19
  9.0 31.5 %collective-permute-start.3 = (f32[16,256]{1,0:T(8,128)S(1)}, f32[16,256]{1,0:T(8,128)S(1)}, u32[]{:S(2)}, u32[]{:S(2)}) collective-permute-start(f32[16,256]{1,0:T(8,128)S(1)} %maximum_maximum_fusion), channel_id=1, source_target_pairs={{0,2},{1,3},{2,4},{3,5},{4,6},{5,7},{6,8},{7,9},{8,10},{9,11},{10,... | collective-permute-start | bytes 49160 | tf_op jit(solution)/shard_map/ppermute | solution.py:19
  9.0 31.4 %collective-permute-start.2 = (f32[16,256]{1,0:T(8,128)S(1)}, f32[16,256]{1,0:T(8,128)S(1)}, u32[]{:S(2)}, u32[]{:S(2)}) collective-permute-start(f32[16,256]{1,0:T(8,128)S(1)} %maximum_maximum_fusion), channel_id=1, source_target_pairs={{0,14},{1,15},{2,0},{3,1},{4,2},{5,3},{6,4},{7,5},{8,6},{9,7},{10,... | collective-permute-start | bytes 49160 | tf_op jit(solution)/shard_map/ppermute | solution.py:19
  14.3 50.4 %collective-permute-start = (bf16[1,192,2048]{2,1,0:T(8,128)(2,1)S(1)}, bf16[1,192,2048]{2,1,0:T(8,128)(2,1)S(1)}, u32[]{:S(2)}, u32[]{:S(2)}) collective-permute-start(bf16[1,192,2048]{2,1,0:T(8,128)(2,1)S(1)} %get-tuple-element.44), channel_id=1, source_target_pairs={{0,1},{1,0},{2,3},{3,2},{4,5},{5,4},{6,7},{7,6},{8,9},{9,8},{10,11... | collective-permute-start | bytes 2359304 | tf_op jit(solution)/shard_map/ppermute | solution.py:19
  23.9 15.9 %copy-start.21 = (s32[256,6]{0,1:T(8,128)S(1)}, s32[256,6]{0,1:T(8,128)}, u32[]{:S(2)}) copy-start(s32[256,6]{0,1:T(8,128)} %param.14) | copy-start | bytes 18436
  23.9 15.9 %copy-start.22 = (s32[256,6]{0,1:T(8,128)S(1)}, s32[256,6]{0,1:T(8,128)}, u32[]{:S(2)}) copy-start(s32[256,6]{0,1:T(8,128)} %param.12) | copy-start | bytes 18436
  43.0 4.9 %collective-permute-start.9 = (f32[16,256]{1,0:T(8,128)S(1)}, f32[16,256]{1,0:T(8,128)S(1)}, u32[]{:S(2)}, u32[]{:S(2)}) collective-permute-start(f32[16,256]{1,0:T(8,128)S(1)} %collective-permute-done.3), channel_id=1, source_target_pairs={{0,2},{1,3},{2,4},{3,5},{4,6},{5,7},{6,8},{7,9},{8,10},{9,11},{10,... | collective-permute-start | bytes 49160 | tf_op jit(solution)/shard_map/ppermute | solution.py:19
  43.0 5.0 %collective-permute-start.8 = (f32[16,256]{1,0:T(8,128)S(1)}, f32[16,256]{1,0:T(8,128)S(1)}, u32[]{:S(2)}, u32[]{:S(2)}) collective-permute-start(f32[16,256]{1,0:T(8,128)S(1)} %collective-permute-done.2), channel_id=1, source_target_pairs={{0,14},{1,15},{2,0},{3,1},{4,2},{5,3},{6,4},{7,5},{8,6},{9,7},{10,... | collective-permute-start | bytes 49160 | tf_op jit(solution)/shard_map/ppermute | solution.py:19
  50.5 4.9 %collective-permute-start.14 = (f32[16,256]{1,0:T(8,128)S(1)}, f32[16,256]{1,0:T(8,128)S(1)}, u32[]{:S(2)}, u32[]{:S(2)}) collective-permute-start(f32[16,256]{1,0:T(8,128)S(1)} %collective-permute-done.9), channel_id=1, source_target_pairs={{0,2},{1,3},{2,4},{3,5},{4,6},{5,7},{6,8},{7,9},{8,10},{9,11},{10,... | collective-permute-start | bytes 49160 | tf_op jit(solution)/shard_map/ppermute | solution.py:19
  50.5 5.0 %collective-permute-start.13 = (f32[16,256]{1,0:T(8,128)S(1)}, f32[16,256]{1,0:T(8,128)S(1)}, u32[]{:S(2)}, u32[]{:S(2)}) collective-permute-start(f32[16,256]{1,0:T(8,128)S(1)} %collective-permute-done.8), channel_id=1, source_target_pairs={{0,14},{1,15},{2,0},{3,1},{4,2},{5,3},{6,4},{7,5},{8,6},{9,7},{10,... | collective-permute-start | bytes 49160 | tf_op jit(solution)/shard_map/ppermute | solution.py:19
  58.1 5.2 %collective-permute-start.18 = (f32[16,256]{1,0:T(8,128)S(1)}, f32[16,256]{1,0:T(8,128)S(1)}, u32[]{:S(2)}, u32[]{:S(2)}) collective-permute-start(f32[16,256]{1,0:T(8,128)S(1)} %collective-permute-done.14), channel_id=1, source_target_pairs={{0,2},{1,3},{2,4},{3,5},{4,6},{5,7},{6,8},{7,9},{8,10},{9,11},{10,... | collective-permute-start | bytes 49160 | tf_op jit(solution)/shard_map/ppermute | solution.py:19
  89.0 34.4 %collective-permute-start.6 = (bf16[2,192,2048]{2,1,0:T(8,128)(2,1)S(1)}, bf16[2,192,2048]{2,1,0:T(8,128)(2,1)S(1)}, u32[]{:S(2)}, u32[]{:S(2)}) collective-permute-start(bf16[2,192,2048]{2,1,0:T(8,128)(2,1)S(1)} %get-tuple-element.36), channel_id=1, source_target_pairs={{0,1},{1,0},{2,3},{3,2},{4,5},{5,4},{6,7},{7,6},{8,9},{9,8},{10,11... | collective-permute-start | bytes 4718600 | tf_op jit(solution)/shard_map/ppermute | solution.py:19
  89.1 26.8 %collective-permute-start.11 = (bf16[256,2048]{1,0:T(8,128)(2,1)}, bf16[256,2048]{1,0:T(8,128)(2,1)}, u32[]{:S(2)}, u32[]{:S(2)}) collective-permute-start(bf16[256,2048]{1,0:T(8,128)(2,1)} %collective-permute-done.5), channel_id=1, source_target_pairs={{0,2},{1,3},{2,4},{3,5},{4,6},{5,7},{6,8},{7,9},{8,10},{9,11},{10,... | collective-permute-start | bytes 3145736 | tf_op jit(solution)/shard_map/ppermute | solution.py:19
  90.3 25.6 %collective-permute-start.10 = (bf16[256,2048]{1,0:T(8,128)(2,1)}, bf16[256,2048]{1,0:T(8,128)(2,1)}, u32[]{:S(2)}, u32[]{:S(2)}) collective-permute-start(bf16[256,2048]{1,0:T(8,128)(2,1)} %collective-permute-done.4), channel_id=1, source_target_pairs={{0,14},{1,15},{2,0},{3,1},{4,2},{5,3},{6,4},{7,5},{8,6},{9,7},{10,... | collective-permute-start | bytes 3145736 | tf_op jit(solution)/shard_map/ppermute | solution.py:19
  105.3 328.3 %collective-permute-start.1 = (bf16[1,192,2048]{2,1,0:T(8,128)(2,1)}, bf16[1,192,2048]{2,1,0:T(8,128)(2,1)}, u32[]{:S(2)}, u32[]{:S(2)}) collective-permute-start(bf16[1,192,2048]{2,1,0:T(8,128)(2,1)} %bitcast.36), channel_id=1, source_target_pairs={{0,1},{1,0},{2,3},{3,2},{4,5},{5,4},{6,7},{7,6},{8,9},{9,8},{10,11... | collective-permute-start | bytes 2359304 | tf_op jit(solution)/shard_map/ppermute | solution.py:19
  120.1 60.3 %collective-permute-start.12 = (bf16[2,192,2048]{2,1,0:T(8,128)(2,1)}, bf16[2,192,2048]{2,1,0:T(8,128)(2,1)}, u32[]{:S(2)}, u32[]{:S(2)}) collective-permute-start(bf16[2,192,2048]{2,1,0:T(8,128)(2,1)} %get-tuple-element.30), channel_id=1, source_target_pairs={{0,1},{1,0},{2,3},{3,2},{4,5},{5,4},{6,7},{7,6},{8,9},{9,8},{10,11... | collective-permute-start | bytes 4718600 | tf_op jit(solution)/shard_map/ppermute | solution.py:19
  120.1 42.7 %collective-permute-start.16 = (bf16[256,2048]{1,0:T(8,128)(2,1)}, bf16[256,2048]{1,0:T(8,128)(2,1)S(1)}, u32[]{:S(2)}, u32[]{:S(2)}) collective-permute-start(bf16[256,2048]{1,0:T(8,128)(2,1)} %collective-permute-done.11), channel_id=1, source_target_pairs={{0,2},{1,3},{2,4},{3,5},{4,6},{5,7},{6,8},{7,9},{8,10},{9,11},{10,... | collective-permute-start | bytes 3145736 | tf_op jit(solution)/shard_map/ppermute | solution.py:19
  121.7 38.3 %collective-permute-start.15 = (bf16[256,2048]{1,0:T(8,128)(2,1)}, bf16[256,2048]{1,0:T(8,128)(2,1)}, u32[]{:S(2)}, u32[]{:S(2)}) collective-permute-start(bf16[256,2048]{1,0:T(8,128)(2,1)} %collective-permute-done.10), channel_id=1, source_target_pairs={{0,14},{1,15},{2,0},{3,1},{4,2},{5,3},{6,4},{7,5},{8,6},{9,7},{10,... | collective-permute-start | bytes 3145736 | tf_op jit(solution)/shard_map/ppermute | solution.py:19
  158.4 6.3 %copy-start = (bf16[2,4,48,2048]{3,2,1,0:T(8,128)(2,1)}, bf16[2,4,48,2048]{3,2,1,0:T(8,128)(2,1)S(1)}, u32[]{:S(2)}) copy-start(bf16[2,4,48,2048]{3,2,1,0:T(8,128)(2,1)S(1)} %copy.19) | copy-start | bytes 4718596
  159.9 224.5 %collective-permute-start.7 = (bf16[2,192,2048]{2,1,0:T(8,128)(2,1)}, bf16[2,192,2048]{2,1,0:T(8,128)(2,1)}, u32[]{:S(2)}, u32[]{:S(2)}) collective-permute-start(bf16[2,192,2048]{2,1,0:T(8,128)(2,1)} %bitcast.59), channel_id=1, source_target_pairs={{0,1},{1,0},{2,3},{3,2},{4,5},{5,4},{6,7},{7,6},{8,9},{9,8},{10,11... | collective-permute-start | bytes 4718600 | tf_op jit(solution)/shard_map/ppermute | solution.py:19
  161.0 14.4 %collective-permute-start.20 = (bf16[128,2048]{1,0:T(8,128)(2,1)S(1)}, bf16[128,2048]{1,0:T(8,128)(2,1)S(1)}, u32[]{:S(2)}, u32[]{:S(2)}) collective-permute-start(bf16[128,2048]{1,0:T(8,128)(2,1)S(1)} %slice.663), channel_id=1, source_target_pairs={{0,14},{1,15},{2,0},{3,1},{4,2},{5,3},{6,4},{7,5},{8,6},{9,7},{10,... | collective-permute-start | bytes 1572872 | tf_op jit(solution)/shard_map/ppermute | solution.py:19
  162.9 15.5 %collective-permute-start.19 = (bf16[128,2048]{1,0:T(8,128)(2,1)S(1)}, bf16[128,2048]{1,0:T(8,128)(2,1)S(1)}, u32[]{:S(2)}, u32[]{:S(2)}) collective-permute-start(bf16[128,2048]{1,0:T(8,128)(2,1)S(1)} %slice.662), channel_id=1, source_target_pairs={{0,2},{1,3},{2,4},{3,5},{4,6},{5,7},{6,8},{7,9},{8,10},{9,11},{10,... | collective-permute-start | bytes 1572872 | tf_op jit(solution)/shard_map/ppermute | solution.py:19
  179.3 4.5 collective-permute-start.21
  179.9 38.1 %collective-permute-start.17 = (bf16[2,192,2048]{2,1,0:T(8,128)(2,1)S(1)}, bf16[2,192,2048]{2,1,0:T(8,128)(2,1)S(1)}, u32[]{:S(2)}, u32[]{:S(2)}) collective-permute-start(bf16[2,192,2048]{2,1,0:T(8,128)(2,1)S(1)} %get-tuple-element.34), channel_id=1, source_target_pairs={{0,1},{1,0},{2,3},{3,2},{4,5},{5,4},{6,7},{7,6},{8,9},{9,8},{10,11... | collective-permute-start | bytes 4718600 | tf_op jit(solution)/shard_map/ppermute | solution.py:19
  216.7 83.8 %collective-permute-start.24 = (bf16[1,192,2048]{2,1,0:T(8,128)(2,1)S(1)}, bf16[1,192,2048]{2,1,0:T(8,128)(2,1)S(1)}, u32[]{:S(2)}, u32[]{:S(2)}) collective-permute-start(bf16[1,192,2048]{2,1,0:T(8,128)(2,1)S(1)} %bitcast.497), channel_id=1, source_target_pairs={{0,1},{1,0},{2,3},{3,2},{4,5},{5,4},{6,7},{7,6},{8,9},{9,8},{10,11... | collective-permute-start | bytes 2359304 | tf_op jit(solution)/shard_map/ppermute | solution.py:19
  259.1 45.2 %collective-permute-start.23 = (bf16[2,192,2048]{2,1,0:T(8,128)(2,1)}, bf16[2,192,2048]{2,1,0:T(8,128)(2,1)S(1)}, u32[]{:S(2)}, u32[]{:S(2)}) collective-permute-start(bf16[2,192,2048]{2,1,0:T(8,128)(2,1)} %bitcast.109), channel_id=1, source_target_pairs={{0,1},{1,0},{2,3},{3,2},{4,5},{5,4},{6,7},{7,6},{8,9},{9,8},{10,11... | collective-permute-start | bytes 4718600 | tf_op jit(solution)/shard_map/ppermute | solution.py:19
  298.5 36.5 %collective-permute-start.22 = (bf16[2,192,2048]{2,1,0:T(8,128)(2,1)S(1)}, bf16[2,192,2048]{2,1,0:T(8,128)(2,1)S(1)}, u32[]{:S(2)}, u32[]{:S(2)}) collective-permute-start(bf16[2,192,2048]{2,1,0:T(8,128)(2,1)S(1)} %bitcast.496), channel_id=1, source_target_pairs={{0,1},{1,0},{2,3},{3,2},{4,5},{5,4},{6,7},{7,6},{8,9},{9,8},{10,11... | collective-permute-start | bytes 4718600 | tf_op jit(solution)/shard_map/ppermute | solution.py:19
  304.2 26.9 %collective-permute-start.25 = (f32[128,2048]{1,0:T(8,128)S(1)}, f32[128,2048]{1,0:T(8,128)S(1)}, u32[]{:S(2)}, u32[]{:S(2)}) collective-permute-start(f32[128,2048]{1,0:T(8,128)S(1)} %get-tuple-element.37), channel_id=1, source_target_pairs={{0,2},{1,3},{2,4},{3,5},{4,6},{5,7},{6,8},{7,9},{8,10},{9,11},{10,... | collective-permute-start | bytes 3145736 | tf_op jit(solution)/shard_map/ppermute | solution.py:19
  304.3 26.7 %collective-permute-start.29 = (f32[128,2048]{1,0:T(8,128)S(1)}, f32[128,2048]{1,0:T(8,128)S(1)}, u32[]{:S(2)}, u32[]{:S(2)}) collective-permute-start(f32[128,2048]{1,0:T(8,128)S(1)} %get-tuple-element.38), channel_id=1, source_target_pairs={{0,14},{1,15},{2,0},{3,1},{4,2},{5,3},{6,4},{7,5},{8,6},{9,7},{10,... | collective-permute-start | bytes 3145736 | tf_op jit(solution)/shard_map/ppermute | solution.py:19
  311.9 23.1 %slice-start.3 = ((s8[9437184]{0:T(1024)(128)(4,1)}), s8[4194304]{0:T(1024)(128)(4,1)S(1)}, s32[]{:S(2)}) async-start(s8[9437184]{0:T(1024)(128)(4,1)} %bitcast.500), calls=%async_computation.3 | async-start | bytes 8388608
  311.9 23.1 %slice-start.4 = ((s8[9437184]{0:T(1024)(128)(4,1)}), s8[4194304]{0:T(1024)(128)(4,1)S(1)}, s32[]{:S(2)}) async-start(s8[9437184]{0:T(1024)(128)(4,1)} %bitcast.500), calls=%async_computation.4 | async-start | bytes 8388608
  317.8 17.2 %slice-start.5 = ((s8[9437184]{0:T(1024)(128)(4,1)}), s8[1048576]{0:T(1024)(128)(4,1)S(1)}, s32[]{:S(2)}) async-start(s8[9437184]{0:T(1024)(128)(4,1)} %bitcast.500), calls=%async_computation.5 | async-start | bytes 2097152
  331.4 48.5 %collective-permute-start.26 = (f32[256,2048]{1,0:T(8,128)S(1)}, f32[256,2048]{1,0:T(8,128)S(1)}, u32[]{:S(2)}, u32[]{:S(2)}) collective-permute-start(f32[256,2048]{1,0:T(8,128)S(1)} %pad_maximum_fusion.3), channel_id=1, source_target_pairs={{0,2},{1,3},{2,4},{3,5},{4,6},{5,7},{6,8},{7,9},{8,10},{9,11},{10,... | collective-permute-start | bytes 6291464 | tf_op jit(solution)/shard_map/ppermute | solution.py:19
  331.7 48.2 %collective-permute-start.30 = (f32[256,2048]{1,0:T(8,128)S(1)}, f32[256,2048]{1,0:T(8,128)S(1)}, u32[]{:S(2)}, u32[]{:S(2)}) collective-permute-start(f32[256,2048]{1,0:T(8,128)S(1)} %pad_maximum_fusion.4), channel_id=1, source_target_pairs={{0,14},{1,15},{2,0},{3,1},{4,2},{5,3},{6,4},{7,5},{8,6},{9,7},{10,... | collective-permute-start | bytes 6291464 | tf_op jit(solution)/shard_map/ppermute | solution.py:19
  339.5 44.9 %slice-start = ((s8[9437184]{0:T(1024)(128)(4,1)}), s8[4194304]{0:T(1024)(128)(4,1)S(1)}, s32[]{:S(2)}) async-start(s8[9437184]{0:T(1024)(128)(4,1)} %bitcast.498), calls=%async_computation | async-start | bytes 8388608
  339.5 44.9 %slice-start.1 = ((s8[9437184]{0:T(1024)(128)(4,1)}), s8[4194304]{0:T(1024)(128)(4,1)S(1)}, s32[]{:S(2)}) async-start(s8[9437184]{0:T(1024)(128)(4,1)} %bitcast.498), calls=%async_computation.1 | async-start | bytes 8388608
  345.2 39.2 %slice-start.2 = ((s8[9437184]{0:T(1024)(128)(4,1)}), s8[1048576]{0:T(1024)(128)(4,1)S(1)}, s32[]{:S(2)}) async-start(s8[9437184]{0:T(1024)(128)(4,1)} %bitcast.498), calls=%async_computation.2 | async-start | bytes 2097152
  381.0 47.6 %collective-permute-start.27 = (f32[256,2048]{1,0:T(8,128)S(1)}, f32[256,2048]{1,0:T(8,128)S(1)}, u32[]{:S(2)}, u32[]{:S(2)}) collective-permute-start(f32[256,2048]{1,0:T(8,128)S(1)} %get-tuple-element.19), channel_id=1, source_target_pairs={{0,2},{1,3},{2,4},{3,5},{4,6},{5,7},{6,8},{7,9},{8,10},{9,11},{10,... | collective-permute-start | bytes 6291464 | tf_op jit(solution)/shard_map/ppermute | solution.py:19
  383.2 45.7 %collective-permute-start.31 = (f32[256,2048]{1,0:T(8,128)S(1)}, f32[256,2048]{1,0:T(8,128)S(1)}, u32[]{:S(2)}, u32[]{:S(2)}) collective-permute-start(f32[256,2048]{1,0:T(8,128)S(1)} %get-tuple-element.20), channel_id=1, source_target_pairs={{0,14},{1,15},{2,0},{3,1},{4,2},{5,3},{6,4},{7,5},{8,6},{9,7},{10,... | collective-permute-start | bytes 6291464 | tf_op jit(solution)/shard_map/ppermute | solution.py:19
  392.2 40.6 %copy-start.24 = (f32[256,6]{0,1:T(8,128)S(1)}, f32[256,6]{0,1:T(8,128)}, u32[]{:S(2)}) copy-start(f32[256,6]{0,1:T(8,128)} %param.13) | copy-start | bytes 18436
  392.2 40.6 %copy-start.23 = (s32[1,256,6]{1,2,0:T(8,128)S(1)}, s32[1,256,6]{1,2,0:T(8,128)}, u32[]{:S(2)}) copy-start(s32[1,256,6]{1,2,0:T(8,128)} %fusion.242) | copy-start | bytes 18436
  392.3 41.3 %copy-start.2 = (bf16[1,4,48,2048]{3,2,0,1:T(8,128)(2,1)S(1)}, bf16[1,4,48,2048]{3,2,0,1:T(8,128)(2,1)}, u32[]{:S(2)}) copy-start(bf16[1,4,48,2048]{3,2,0,1:T(8,128)(2,1)} %get-tuple-element.40) | copy-start | bytes 2359300
  430.1 45.5 %collective-permute-start.32 = (f32[256,2048]{1,0:T(8,128)S(1)}, f32[256,2048]{1,0:T(8,128)S(1)}, u32[]{:S(2)}, u32[]{:S(2)}) collective-permute-start(f32[256,2048]{1,0:T(8,128)S(1)} %get-tuple-element.18), channel_id=1, source_target_pairs={{0,14},{1,15},{2,0},{3,1},{4,2},{5,3},{6,4},{7,5},{8,6},{9,7},{10,... | collective-permute-start | bytes 6291464 | tf_op jit(solution)/shard_map/ppermute | solution.py:19
  432.8 46.1 %collective-permute-start.28 = (f32[256,2048]{1,0:T(8,128)S(1)}, f32[256,2048]{1,0:T(8,128)S(1)}, u32[]{:S(2)}, u32[]{:S(2)}) collective-permute-start(f32[256,2048]{1,0:T(8,128)S(1)} %get-tuple-element.17), channel_id=1, source_target_pairs={{0,2},{1,3},{2,4},{3,5},{4,6},{5,7},{6,8},{7,9},{8,10},{9,11},{10,... | collective-permute-start | bytes 6291464 | tf_op jit(solution)/shard_map/ppermute | solution.py:19
  434.8 44.2 %copy-start.6 = (f32[256,2048]{1,0:T(8,128)S(1)}, f32[256,2048]{1,0:T(8,128)}, u32[]{:S(2)}) copy-start(f32[256,2048]{1,0:T(8,128)} %fusion.107) | copy-start | bytes 6291460
  (19 other events, 53.4 us)

commit v2 on v0

v2 whole, which is shorter than its diff:
```python
import functools

import jax
import jax.numpy as jnp
from jax import lax
from jax.experimental import pallas as pl
from jax.experimental.pallas import tpu as pltpu
from jax.sharding import PartitionSpec as P

MESH = pl.DeviceIdType.MESH
F32 = jnp.float32
BF16 = jnp.bfloat16


def chunks(total, width):
    return [(start, min(width, total - start)) for start in range(0, total, width)]


def moe_kernel(num_ep, top_k, capacity,
               tok_hbm, meta_hbm, gate_ref, ws1, ws3, ws2, we1, we3, we2,
               out_ref,
               tok, meta, w1a, w1b, w3a, w3b, w2s, xbuf, xsend, rbuf, rrecv, hbuf, part, rs, base,
               load_sem, ab_sem, w2_sem,
               first_send, first_recv, second_send, second_recv, meta_send, meta_recv,
               x_send, x_recv, r_send, r_recv, rs_send, rs_recv, credit):
    tokens, hidden = tok.shape[1:]
    experts = we1.shape[0]
    ff = we1.shape[2]
    ff_a, ff_b = w1a.shape[1], w1b.shape[1]
    half_tok = tokens // 2
    nz = num_ep // 2
    far = nz // 2
    core_rows = experts * capacity
    chip_rows = 2 * core_rows
    pieces = 4
    piece = tokens // pieces
    quarter = half_tok // 2

    ep = lax.axis_index('ep')
    z, core = ep // 2, ep % 2
    right = (ep + 2) % num_ep
    left = (ep + num_ep - 2) % num_ep
    partner = z * 2 + 1 - core
    towards = (right, left)
    origin = (left, right)

    barrier = pltpu.get_barrier_semaphore()
    for other in (left, right, partner):
        pl.semaphore_signal(barrier, inc=1, device_id={'ep': other}, device_id_type=MESH)

    load_tok = pltpu.make_async_copy(tok_hbm, tok.at[0], load_sem.at[0])
    load_meta = pltpu.make_async_copy(meta_hbm, meta.at[0], load_sem.at[1])
    load_tok.start()
    load_meta.start()

    def ab_copies(which, m1, m3, lead, col):
        lo, width = (0, ff_a) if which == 0 else (ff_a, ff_b)
        dst1, dst3 = (w1a, w3a) if which == 0 else (w1b, w3b)
        cols = pl.ds(col + lo, width)
        src1 = m1.at[lead, :, cols] if lead is not None else m1.at[:, cols]
        src3 = m3.at[lead, :, cols] if lead is not None else m3.at[:, cols]
        return (pltpu.make_async_copy(src1, dst1, ab_sem.at[which, 0]),
                pltpu.make_async_copy(src3, dst3, ab_sem.at[which, 1]))

    def start_ab(which, e):
        for c in ab_copies(which, we1, we3, e, 0):
            c.start()

    def start_shared_ab(which, i):
        for c in ab_copies(which, ws1, ws3, None, i * ff):
            c.start()

    def wait_ab(which):
        for c in ab_copies(which, we1, we3, 0, 0):
            c.wait()

    def w2_copy(e, slot):
        return pltpu.make_async_copy(we2.at[e], w2s.at[slot], w2_sem.at[slot])

    def shared_w2_copy(i, slot):
        return pltpu.make_async_copy(ws2.at[pl.ds(i * ff, ff)], w2s.at[slot], w2_sem.at[slot])

    start_ab(0, 0)
    start_ab(1, 0)
    w2_copy(0, 0).start()
    w2_copy(1, 1).start()
    load_tok.wait()
    load_meta.wait()
    pl.semaphore_wait(barrier, 3)

    def slot_of(direction, d):
        if d == 0:
            return 0
        if d == far:
            return 2 * far - 1
        return d if direction == 0 else far - 1 + d

    def remote(src, dst, send_sem, recv_sem, device):
        return pltpu.make_async_remote_copy(src_ref=src, dst_ref=dst, send_sem=send_sem, recv_sem=recv_sem,
                                            device_id={'ep': device}, device_id_type=MESH)

    def first_copy(direction, d, q):
        rows = pl.ds((0 if direction == 0 else half_tok) + q * quarter, quarter)
        return remote(tok.at[slot_of(direction, d - 1), rows], tok.at[slot_of(direction, d), rows],
                      first_send.at[direction, d - 1, q], first_recv.at[direction, d - 1, q], towards[direction])

    def second_copy(direction, d):
        rows = pl.ds(half_tok if direction == 0 else 0, half_tok)
        return remote(tok.at[slot_of(direction, d - 1), rows], tok.at[slot_of(direction, d), rows],
                      second_send.at[direction, d - 1], second_recv.at[direction, d - 1], towards[direction])

    def meta_copy(direction, d):
        return remote(meta.at[slot_of(direction, d - 1)], meta.at[slot_of(direction, d)],
                      meta_send.at[direction, d - 1], meta_recv.at[direction, d - 1], towards[direction])

    def meta_hops(direction):
        return far if direction == 0 else far - 1

    for direction in (0, 1):
        meta_copy(direction, 1).start()
        for q in (0, 1):
            first_copy(direction, 1, q).start()
    for d in range(1, far):
        for direction in (0, 1):
            meta_copy(direction, d).wait_recv()
            if d + 1 <= meta_hops(direction):
                meta_copy(direction, d + 1).start()
        for q in (0, 1):
            for direction in (0, 1):
                first_copy(direction, d, q).wait_recv()
                first_copy(direction, d + 1, q).start()
    for direction in (0, 1):
        second_copy(direction, 1).start()
    meta_copy(0, far).wait_recv()
    for q in (0, 1):
        for direction in (0, 1):
            first_copy(direction, far, q).wait_recv()

    def second_step(d):
        for direction in (0, 1):
            second_copy(direction, d).wait_recv()
            if d + 1 < far:
                second_copy(direction, d + 1).start()

    my_base = (z * chip_rows).astype(F32)
    my_core = (core * core_rows).astype(F32)

    def relative(slot):
        code = meta[slot, 0:top_k, :]
        rel = code - my_base
        inside = (code >= 0.0) & (rel >= 0.0) & (rel < float(chip_rows))
        rel = rel - my_core
        rel = jnp.where(rel < 0.0, rel + float(chip_rows), rel)
        return jnp.where(inside, rel, -1.0)

    def position():
        return lax.broadcasted_iota(jnp.int32, (chip_rows, tokens), 0).astype(F32)

    def gather(i, slot):
        rel = relative(slot)
        pos = position()
        sel = jnp.zeros((chip_rows, tokens), F32)
        for k in range(top_k):
            sel = jnp.where(pos == rel[k:k + 1, :], 1.0, sel)
        sel = sel.astype(BF16)
        for n0, nw in chunks(hidden, 512):
            rows = jnp.dot(sel, tok[slot, :, n0:n0 + nw], preferred_element_type=F32).astype(BF16)
            xbuf[i, :, n0:n0 + nw] = rows[:core_rows]
            xsend[i, :, n0:n0 + nw] = rows[core_rows:]

    def combine(i, slot, dst):
        rel = relative(slot)
        gates = meta[slot, top_k:2 * top_k, :]
        pos = position()
        w = jnp.zeros((chip_rows, tokens), F32)
        for k in range(top_k):
            w = jnp.where(pos == rel[k:k + 1, :], gates[k:k + 1, :], w)
        w = w.T
        hi = w.astype(BF16)
        rest = w - hi.astype(F32)
        mid = rest.astype(BF16)
        low = (rest - mid.astype(F32)).astype(BF16)
        for n0, nw in chunks(hidden, 256):
            res = jnp.concatenate([rbuf[i, :, n0:n0 + nw], rrecv[i, :, n0:n0 + nw]], axis=0)
            acc = jnp.dot(hi, res, preferred_element_type=F32)
            acc = acc + jnp.dot(mid, res, preferred_element_type=F32)
            acc = acc + jnp.dot(low, res, preferred_element_type=F32)
            dst[:, n0:n0 + nw] = acc

    def up_half(x_of, rows, which):
        lo, width = (0, ff_a) if which == 0 else (ff_a, ff_b)
        m1, m3 = (w1a, w3a) if which == 0 else (w1b, w3b)
        x = x_of()
        for n0, nw in chunks(width, 256):
            a = jnp.dot(x, m1[:, n0:n0 + nw], preferred_element_type=F32)
            b = jnp.dot(x, m3[:, n0:n0 + nw], preferred_element_type=F32)
            hbuf[0:rows, lo + n0:lo + n0 + nw] = (jax.nn.silu(a) * b).astype(BF16)

    def expert_loop(phase_srcs, last, extra):
        rows = capacity * len(phase_srcs)

        def body(e, carry):
            row0 = pl.multiple_of(e * capacity, 16)
            nxt = (e + 1) % experts

            def x_of():
                return jnp.concatenate([xbuf[s, pl.ds(row0, capacity), :] for s in phase_srcs], axis=0)

            for which in (0, 1):
                wait_ab(which)
                up_half(x_of, rows, which)
                if last:
                    @pl.when(e < experts - 1)
                    def _():
                        start_ab(which, nxt)

                    @pl.when(e == experts - 1)
                    def _():
                        start_shared_ab(which, 0)
                else:
                    start_ab(which, nxt)
            slot = e % 2
            w2_copy(0, slot).wait()
            for n0, nw in chunks(hidden, 256):
                r = jnp.dot(hbuf[0:rows, :], w2s[slot, :, n0:n0 + nw], preferred_element_type=F32).astype(BF16)
                for j, s in enumerate(phase_srcs):
                    rbuf[s, pl.ds(row0, capacity), n0:n0 + nw] = r[j * capacity:(j + 1) * capacity]
            if last:
                @pl.when(e < experts - 2)
                def _():
                    w2_copy(e + 2, slot).start()

                for i in (0, 1):
                    @pl.when(e == experts - 2 + i)
                    def _():
                        shared_w2_copy(i, i).start()
            else:
                w2_copy((e + 2) % experts, slot).start()
            if extra is not None:
                extra(e)
            return carry

        lax.fori_loop(0, experts, body, 0)

    def x_copy(phase, n):
        return remote(xsend.at[pl.ds(0, n)], xbuf.at[pl.ds(2, n)], x_send.at[phase], x_recv.at[phase], partner)

    def r_copy(phase, n):
        return remote(rbuf.at[pl.ds(2, n)], rrecv.at[pl.ds(0, n)], r_send.at[phase], r_recv.at[phase], partner)

    def run_phase(phase, slots, dsts, last=False, extra=None, before_combine=None):
        n = len(slots)
        for i, slot in enumerate(slots):
            gather(i, slot)
        x_copy(phase, n).start()
        x_copy(phase, n).wait()
        expert_loop([0, 2] if n == 1 else [0, 1, 2, 3], last, extra)
        r_copy(phase, n).start()
        r_copy(phase, n).wait()
        if before_combine is not None:
            before_combine()
        for i, slot in enumerate(slots):
            combine(i, slot, dsts[i])

    def rs_copy(direction, hop, rows_piece):
        rows = pl.ds(pl.multiple_of(rows_piece * piece, 8), piece)
        if hop == 1:
            src = part.at[0, 0, rows]
        else:
            src = part.at[(hop - 1) % 2, direction, rows]
        return remote(src, rs.at[direction, (hop - 1) % 2, rows],
                      rs_send.at[direction, hop - 1, rows_piece], rs_recv.at[direction, hop - 1, rows_piece],
                      towards[direction])

    def first_pieces(direction):
        return (0, 1) if direction == 0 else (2, 3)

    def forward(direction, hop, p, add):
        rows = pl.ds(pl.multiple_of(p * piece, 8), piece)
        if add:
            rs_copy(direction, hop - 1, p).wait_recv()
            mine = part.at[(hop - 1) % 2, direction, rows]
            mine[...] = mine[...] + rs[direction, hop % 2, rows, :]
        rs_copy(direction, hop, p).start()

    def give_credit(which):
        for direction in (0, 1):
            pl.semaphore_signal(credit.at[direction, which], inc=1, device_id={'ep': origin[direction]}, device_id_type=MESH)

    def take_credit(which):
        for direction in (0, 1):
            pl.semaphore_wait(credit.at[direction, which], 1)

    def wait_sends(hop):
        for direction in (0, 1):
            for p in (first_pieces(direction) if hop == 1 else range(pieces)):
                rs_copy(direction, hop, p).wait_send()

    def gather_service(e):
        for step in range(1, far - 1):
            @pl.when(e == 2 * (step - 1))
            def _():
                second_step(step)

    run_phase(0, [slot_of(0, far)], [part.at[0, 0]], extra=gather_service)
    for direction in (0, 1):
        for p in first_pieces(direction):
            rs_copy(direction, 1, p).start()
    second_step(far - 1)

    def pair(d):
        return [slot_of(1, d), slot_of(0, d)]

    run_phase(1, pair(far - 1), [part.at[1, 0], part.at[1, 1]])
    for j in (0, 1):
        for direction in (0, 1):
            forward(direction, 2, first_pieces(direction)[j], True)
    give_credit(0)
    for j in (0, 1):
        for direction in (0, 1):
            forward(direction, 2, first_pieces(1 - direction)[j], False)

    run_phase(2, pair(far - 2), [part.at[0, 0], part.at[0, 1]], before_combine=lambda: wait_sends(1))
    take_credit(0)

    def service(hop):
        def run(e):
            for direction in (0, 1):
                forward(direction, hop, e, True)
        return run

    run_phase(3, pair(far - 3), [part.at[1, 0], part.at[1, 1]], extra=service(3), before_combine=lambda: wait_sends(2))
    give_credit(1)
    take_credit(1)

    run_phase(4, [0], [base], last=True, extra=service(4))

    x_all = tok[0].astype(F32) * gate_ref[...].astype(F32)
    scale = jax.nn.sigmoid(jnp.sum(x_all, axis=1, keepdims=True))

    def shared_body(i, carry):
        for which in (0, 1):
            wait_ab(which)
            up_half(lambda: tok[0], tokens, which)

            @pl.when(i == 0)
            def _():
                start_shared_ab(which, 1)
        w2_copy(0, i).wait()
        for n0, nw in chunks(hidden, 256):
            s = jnp.dot(hbuf[0:tokens, :], w2s[i, :, n0:n0 + nw], preferred_element_type=F32)
            base[:, n0:n0 + nw] = base[:, n0:n0 + nw] + scale * s
        return carry

    lax.fori_loop(0, 2, shared_body, 0)

    def finish(p, carry):
        rows = pl.ds(pl.multiple_of(p * piece, 16), piece)
        total = tok[0, rows, :].astype(F32) + base[rows, :]
        for direction in (0, 1):
            rs_copy(direction, far, p).wait_recv()
            total = total + rs[direction, (far - 1) % 2, rows, :]
        out_ref[rows, :] = total.astype(BF16)
        return carry

    lax.fori_loop(0, pieces, finish, 0)

    for direction in (0, 1):
        for d in range(1, far + 1):
            for q in (0, 1):
                first_copy(direction, d, q).wait_send()
            if d < far:
                second_copy(direction, d).wait_send()
            if d <= meta_hops(direction):
                meta_copy(direction, d).wait_send()
    wait_sends(3)
    wait_sends(4)


def solution(mesh):
    num_ep = mesh.shape['ep']
    row_spec = P(('dp', 'ep'), None)
    replicated = P()
    expert_spec = P('ep', None, None)

    def device_step(tokens, expert_ids, gate_vals, slots, shared_w1, shared_w3, shared_w2, shared_gate, expert_w1, expert_w3, expert_w2):
        tok_count, hidden = tokens.shape
        top_k = expert_ids.shape[1]
        experts, _, ff = expert_w1.shape
        num_experts = experts * num_ep
        capacity = 8 * ((2 * tok_count * top_k + 8 * num_experts - 1) // (8 * num_experts))
        core_rows = experts * capacity
        far = num_ep // 4
        ff_a = 256 * ((ff + 511) // 512)
        ff_b = ff - ff_a

        code = jnp.where(slots >= 0, expert_ids * capacity + slots, -1).astype(F32)
        meta = jnp.concatenate([code, gate_vals, jnp.zeros((tok_count, 16 - 2 * top_k), F32)], axis=1).T

        vmem = pl.BlockSpec(memory_space=pltpu.VMEM)
        hbm = pl.BlockSpec(memory_space=pl.ANY)
        dma = pltpu.SemaphoreType.DMA
        return pl.pallas_call(
            functools.partial(moe_kernel, num_ep, top_k, capacity),
            out_shape=jax.ShapeDtypeStruct((tok_count, hidden), BF16),
            in_specs=[hbm, hbm, vmem] + [hbm] * 6,
            out_specs=vmem,
            scratch_shapes=[
                pltpu.VMEM((2 * far, tok_count, hidden), BF16),
                pltpu.VMEM((2 * far, 16, tok_count), F32),
                pltpu.VMEM((hidden, ff_a), BF16),
                pltpu.VMEM((hidden, ff_b), BF16),
                pltpu.VMEM((hidden, ff_a), BF16),
                pltpu.VMEM((hidden, ff_b), BF16),
                pltpu.VMEM((2, ff, hidden), BF16),
                pltpu.VMEM((4, core_rows, hidden), BF16),
                pltpu.VMEM((2, core_rows, hidden), BF16),
                pltpu.VMEM((4, core_rows, hidden), BF16),
                pltpu.VMEM((2, core_rows, hidden), BF16),
                pltpu.VMEM((tok_count, ff), BF16),
                pltpu.VMEM((2, 2, tok_count, hidden), F32),
                pltpu.VMEM((2, 2, tok_count, hidden), F32),
                pltpu.VMEM((tok_count, hidden), F32),
                dma((2,)), dma((2, 2)), dma((2,)),
                dma((2, far, 2)), dma((2, far, 2)), dma((2, far)), dma((2, far)), dma((2, far)), dma((2, far)),
                dma((far + 1,)), dma((far + 1,)), dma((far + 1,)), dma((far + 1,)),
                dma((2, far, 4)), dma((2, far, 4)), pltpu.SemaphoreType.REGULAR((2, 2)),
            ],
            compiler_params=pltpu.CompilerParams(collective_id=0, has_side_effects=True, vmem_limit_bytes=66_000_000),
        )(tokens, meta, shared_gate.reshape(1, hidden), shared_w1, shared_w3, shared_w2, expert_w1, expert_w3, expert_w2)

    return jax.shard_map(device_step, mesh=mesh, in_specs=(row_spec, row_spec, row_spec, row_spec, replicated, replicated, replicated, replicated, expert_spec, expert_spec, expert_spec), out_specs=row_spec, check_vma=False)
```

time: 772 us -> 274 us (0.35)
  blocking collectives: 287 us -> 0 us
  waiting for transfers between devices: 274 us -> 0 us
  Pallas kernels: 0 us -> 268 us
  matrix products: 114 us -> 0 us
  local copies, waits for them, and re-layouts: 73 us -> 3.67 us
  other arithmetic: 18.3 us -> 2.09 us
    all_to_all x1 -> x0, blocking collectives: 287 us -> none  [device_step(): lax.all_to_all(send_buf.reshape(num_ep, local_experts * capacity, hidden)...]
    all_to_all x1 -> x0, waiting for transfers between devices: 274 us -> none  [device_step(): lax.all_to_all(expert_out.reshape(num_ep, local_experts * capacity, hidde...]
    pallas_call x0 -> x1, Pallas kernels: none -> 268 us  [device_step(): pl.pallas_call(functools.partial(moe_kernel, num_ep, top_k, capacity), ou...]
    dot_general x6 -> x0, matrix products: 114 us -> none  [the longest x1 32.3 us: device_step(): jnp.einsum('secd,edf->secf', expert_in, expert_w1, preferred_element_type...]
    gather x3 -> x0, local copies, waits for them, and re-layouts: 55.1 us -> none  [the longest x2 29.9 us: device_step(): jnp.take(back_buf.reshape(buf_rows, hidden), slot_dest, axis=0, mode='fil...]
    convert_element_type x1 -> x0, local copies, waits for them, and re-layouts: 10.7 us -> none  [device_step(): jnp.einsum('secf,efd->secd', hidden_act, expert_w2, preferred_element_typ...]
    reduce_sum x1 -> x0, other arithmetic: 10.6 us -> none  [device_step(): routed = jnp.sum(weights * picked, axis=1)]
  transfers between devices with their start and end apart: 1 -> 0, of which waited for: 1 -> 0; matrix products, arithmetic and copies ran while one was open for 1% -> 0% of each run, Pallas kernels for 0% -> 0%
where the time goes in v2:
time: 274 us
  Pallas kernels  268 us (98%)
  local copies, waits for them, and re-layouts  3.67 us (1%)
    pallas_call x1, Pallas kernels, device_step(): pl.pallas_call(functools.partial(moe_kernel, num_ep, top_k, capacity), ou...  268 us

profile of v2, /device:TPU:21, one launch (start us, length us, event | category | flops | bytes accessed | tf_op | source)
XLA Modules:
  0.0 274.0 jit_solution(14848550456691855098)
XLA Ops:
  0.0 0.1 pad.2.clone
  0.1 0.7 select_convert_fusion
  0.8 1.4 maximum_bitcast_fusion.meta_hbm
  2.2 1.3 reshape.3.gate_ref
  3.5 268.3 %shard_map.109 = bf16[256,2048]{1,0:T(8,128)(2,1)} custom-call(bf16[256,2048]{1,0:T(8,128)(2,1)} %tok_hbm.1, f32[16,256]{1,0:T(8,128)} %maximum_bitcast_fusion.meta_hbm, bf16[1,2048]{1,0:T(2,128)(2,1)} %reshape.3.gate_ref, bf16[2048,2816]{1,0:T(8,128)(2,1)} %ws1.1, bf16[2048,2816]{1,0:T(8,128)(2,1)} %ws3.1, bf16[2816,2048]{1,0:T(8,128)(2,1)} %ws2.1, ...), custom_call_target="tpu_custom_call" | custom-call | tf_op jit(solution)/shard_map/pallas_call | solution.py:403
  271.7 2.3 copy.13
  (1 shorter events, 0.0 us)

commit v3 on v2

v3 whole, which is shorter than its diff:
```python
import functools

import jax
import jax.numpy as jnp
from jax import lax
from jax.experimental import pallas as pl
from jax.experimental.pallas import tpu as pltpu
from jax.sharding import PartitionSpec as P

MESH = pl.DeviceIdType.MESH
F32 = jnp.float32
BF16 = jnp.bfloat16


def chunks(total, width):
    return [(start, min(width, total - start)) for start in range(0, total, width)]


def moe_kernel(num_ep, capacity,
               tok_hbm, ids_ref, slots_ref, gates_ref, gate_ref, ws1, ws3, ws2, we1, we3, we2,
               out_ref,
               tok, meta, w1a, w1b, w3a, w3b, w2s, xbuf, xsend, rbuf, rrecv, hbuf, part, rs, base,
               load_sem, ab_sem, w2_sem,
               first_send, first_recv, second_send, second_recv, meta_send, meta_recv,
               x_send, x_recv, r_send, r_recv, rs_send, rs_recv, credit):
    scope = jax.named_scope
    tokens, hidden = tok.shape[1:]
    top_k = ids_ref.shape[0]
    experts = we1.shape[0]
    ff = we1.shape[2]
    ff_a, ff_b = w1a.shape[1], w1b.shape[1]
    half_tok = tokens // 2
    nz = num_ep // 2
    far = nz // 2
    core_rows = experts * capacity
    chip_rows = 2 * core_rows
    pieces = rs_send.shape[2]
    width = hidden // pieces
    firsts = first_send.shape[2]
    first_rows = half_tok // firsts
    seconds = second_send.shape[2]
    second_rows = half_tok // seconds

    ep = lax.axis_index('ep')
    z, core = ep // 2, ep % 2
    right = (ep + 2) % num_ep
    left = (ep + num_ep - 2) % num_ep
    partner = z * 2 + 1 - core
    towards = (right, left)
    origin = (left, right)
    both = (0, 1)

    barrier = pltpu.get_barrier_semaphore()
    for other in (left, right, partner):
        pl.semaphore_signal(barrier, inc=1, device_id={'ep': other}, device_id_type=MESH)

    load_tok = pltpu.make_async_copy(tok_hbm, tok.at[0], load_sem.at[0])
    load_tok.start()
    meta[0, 0:top_k, :] = jnp.where(slots_ref[...] >= 0, ids_ref[...] * capacity + slots_ref[...], -1).astype(F32)
    meta[0, 8:8 + top_k, :] = gates_ref[...]

    def ab_copies(which, m1, m3, lead, col):
        lo, span = (0, ff_a) if which == 0 else (ff_a, ff_b)
        dst1, dst3 = (w1a, w3a) if which == 0 else (w1b, w3b)
        cols = pl.ds(col + lo, span)
        src1 = m1.at[lead, :, cols] if lead is not None else m1.at[:, cols]
        src3 = m3.at[lead, :, cols] if lead is not None else m3.at[:, cols]
        return (pltpu.make_async_copy(src1, dst1, ab_sem.at[which, 0]),
                pltpu.make_async_copy(src3, dst3, ab_sem.at[which, 1]))

    def start_ab(which, e):
        for c in ab_copies(which, we1, we3, e, 0):
            c.start()

    def start_shared_ab(which, i):
        for c in ab_copies(which, ws1, ws3, None, i * ff):
            c.start()

    def wait_ab(which):
        for c in ab_copies(which, we1, we3, 0, 0):
            c.wait()

    def w2_copy(e, slot):
        return pltpu.make_async_copy(we2.at[e], w2s.at[slot], w2_sem.at[slot])

    def shared_w2_copy(i, slot):
        return pltpu.make_async_copy(ws2.at[pl.ds(i * ff, ff)], w2s.at[slot], w2_sem.at[slot])

    def slot_of(direction, d):
        if d == 0:
            return 0
        if d == far:
            return 2 * far - 1
        return d if direction == 0 else far - 1 + d

    def remote(src, dst, send_sem, recv_sem, device):
        return pltpu.make_async_remote_copy(src_ref=src, dst_ref=dst, send_sem=send_sem, recv_sem=recv_sem,
                                            device_id={'ep': device}, device_id_type=MESH)

    def first_copy(direction, d, q):
        rows = pl.ds((0 if direction == 0 else half_tok) + q * first_rows, first_rows)
        return remote(tok.at[slot_of(direction, d - 1), rows], tok.at[slot_of(direction, d), rows],
                      first_send.at[direction, d - 1, q], first_recv.at[direction, d - 1, q], towards[direction])

    def second_copy(direction, d, q):
        rows = pl.ds((half_tok if direction == 0 else 0) + q * second_rows, second_rows)
        return remote(tok.at[slot_of(direction, d - 1), rows], tok.at[slot_of(direction, d), rows],
                      second_send.at[direction, d - 1, q], second_recv.at[direction, d - 1, q], towards[direction])

    def meta_copy(direction, d):
        return remote(meta.at[slot_of(direction, d - 1)], meta.at[slot_of(direction, d)],
                      meta_send.at[direction, d - 1], meta_recv.at[direction, d - 1], towards[direction])

    def meta_hops(direction):
        return far if direction == 0 else far - 1

    with scope('load'):
        load_tok.wait()
    with scope('barrier'):
        pl.semaphore_wait(barrier, 3)
    for q in range(firsts):
        for direction in both:
            first_copy(direction, 1, q).start()
            if q == 0:
                meta_copy(direction, 1).start()
    start_ab(0, 0)
    start_ab(1, 0)
    w2_copy(0, 0).start()
    w2_copy(1, 1).start()
    for d in range(1, far):
        with scope('ag_hop'):
            for q in range(firsts):
                for direction in both:
                    first_copy(direction, d, q).wait_recv()
                    first_copy(direction, d + 1, q).start()
                    if q == 0:
                        meta_copy(direction, d).wait_recv()
                        if d + 1 <= meta_hops(direction):
                            meta_copy(direction, d + 1).start()
    for q in range(seconds):
        for direction in both:
            second_copy(direction, 1, q).start()
    with scope('ag_far'):
        meta_copy(0, far).wait_recv()
        for q in range(firsts):
            for direction in both:
                first_copy(direction, far, q).wait_recv()

    def second_step(d, q):
        with scope('second_step'):
            for direction in both:
                second_copy(direction, d, q).wait_recv()
                if d + 1 < far:
                    second_copy(direction, d + 1, q).start()

    my_base = (z * chip_rows).astype(F32)
    my_core = (core * core_rows).astype(F32)

    def relative(slot):
        code = meta[slot, 0:top_k, :]
        rel = code - my_base
        inside = (code >= 0.0) & (rel >= 0.0) & (rel < float(chip_rows))
        rel = rel - my_core
        rel = jnp.where(rel < 0.0, rel + float(chip_rows), rel)
        return jnp.where(inside, rel, -1.0)

    def position():
        return lax.broadcasted_iota(jnp.int32, (chip_rows, tokens), 0).astype(F32)

    def gather(i, slot):
        rel = relative(slot)
        pos = position()
        sel = jnp.zeros((chip_rows, tokens), F32)
        for k in range(top_k):
            sel = jnp.where(pos == rel[k:k + 1, :], 1.0, sel)
        sel = sel.astype(BF16)
        for n0, nw in chunks(hidden, 512):
            rows = jnp.dot(sel, tok[slot, :, n0:n0 + nw], preferred_element_type=F32).astype(BF16)
            xbuf[i, :, n0:n0 + nw] = rows[:core_rows]
            xsend[i, :, n0:n0 + nw] = rows[core_rows:]

    def weights_of(slot):
        rel = relative(slot)
        gates = meta[slot, 8:8 + top_k, :]
        pos = position()
        w = jnp.zeros((chip_rows, tokens), F32)
        for k in range(top_k):
            w = jnp.where(pos == rel[k:k + 1, :], gates[k:k + 1, :], w)
        w = w.T
        hi = w.astype(BF16)
        rest = w - hi.astype(F32)
        mid = rest.astype(BF16)
        low = (rest - mid.astype(F32)).astype(BF16)
        return hi, mid, low

    def combine(i, terms, dst, p):
        for n0, nw in chunks(width, 256):
            n0 = p * width + n0
            res = jnp.concatenate([rbuf[i, :, n0:n0 + nw], rrecv[i, :, n0:n0 + nw]], axis=0)
            acc = jnp.dot(terms[0], res, preferred_element_type=F32)
            for term in terms[1:]:
                acc = acc + jnp.dot(term, res, preferred_element_type=F32)
            dst[:, n0:n0 + nw] = acc

    def up_part(x_of, rows, which):
        lo, span = (0, ff_a) if which == 0 else (ff_a, ff_b)
        m1, m3 = (w1a, w3a) if which == 0 else (w1b, w3b)
        x = x_of()
        for n0, nw in chunks(span, 256):
            a = jnp.dot(x, m1[:, n0:n0 + nw], preferred_element_type=F32)
            b = jnp.dot(x, m3[:, n0:n0 + nw], preferred_element_type=F32)
            hbuf[0:rows, lo + n0:lo + n0 + nw] = (jax.nn.silu(a) * b).astype(BF16)

    def x_copy(phase, i):
        return remote(xsend.at[i], xbuf.at[2 + i], x_send.at[phase, i], x_recv.at[phase, i], partner)

    def r_copy(phase, e):
        rows = pl.ds(pl.multiple_of(e * capacity, 16), capacity)
        return remote(rbuf.at[pl.ds(2, 2), rows], rrecv.at[:, rows], r_send.at[phase, e], r_recv.at[phase, e], partner)

    def expert_loop(phase, last, extra):
        def body(e, carry):
            row0 = pl.multiple_of(e * capacity, 16)
            nxt = (e + 1) % experts

            def x_of():
                return jnp.concatenate([xbuf[s, pl.ds(row0, capacity), :] for s in range(4)], axis=0)

            for which in both:
                with scope('wait_ab'):
                    wait_ab(which)
                with scope('up'):
                    up_part(x_of, 4 * capacity, which)
                if last:
                    @pl.when(e < experts - 1)
                    def _():
                        start_ab(which, nxt)

                    @pl.when(e == experts - 1)
                    def _():
                        start_shared_ab(which, 0)
                else:
                    start_ab(which, nxt)
                if extra is not None:
                    extra(e, which)
            slot = e % 2
            with scope('wait_w2'):
                w2_copy(0, slot).wait()
            with scope('down'):
                for n0, nw in chunks(hidden, 256):
                    r = jnp.dot(hbuf[0:4 * capacity, :], w2s[slot, :, n0:n0 + nw], preferred_element_type=F32).astype(BF16)
                    for s in range(4):
                        rbuf[s, pl.ds(row0, capacity), n0:n0 + nw] = r[s * capacity:(s + 1) * capacity]
            r_copy(phase, e).start()
            if last:
                @pl.when(e < experts - 2)
                def _():
                    w2_copy(e + 2, slot).start()

                for i in both:
                    @pl.when(e == experts - 2 + i)
                    def _():
                        shared_w2_copy(i, i).start()
            else:
                w2_copy((e + 2) % experts, slot).start()
            if extra is not None:
                extra(e, 2)
            return carry

        with scope('experts'):
            lax.fori_loop(0, experts, body, 0)

    def run_experts(phase, slots, last=False, extra=None):
        with scope('gather'):
            for i in both:
                gather(i, slots[i])
                x_copy(phase, i).start()
        with scope('x_swap'):
            for i in both:
                x_copy(phase, i).wait()
        expert_loop(phase, last, extra)
        with scope('weights'):
            terms = [weights_of(slot) for slot in slots]
        with scope('r_swap'):
            for e in range(experts):
                r_copy(phase, e).wait()
        return terms

    def rs_copy(direction, hop, p):
        cols = pl.ds(p * width if isinstance(p, int) else pl.multiple_of(p * width, 128), width)
        src = part.at[0, 0, :, cols] if hop == 1 else part.at[(hop - 1) % 2, direction, :, cols]
        return remote(src, rs.at[direction, (hop - 1) % 2, :, cols],
                      rs_send.at[direction, hop - 1, p], rs_recv.at[direction, hop - 1, p], towards[direction])

    def first_pieces(direction):
        half = pieces // 2
        return range(0, half) if direction == 0 else range(half, pieces)

    def order(direction, j):
        return (j + pieces // 2) % pieces if direction == 0 else j

    def forward(direction, hop, p, add):
        if add:
            rs_copy(direction, hop - 1, p).wait_recv()
            cols = pl.ds(p * width if isinstance(p, int) else pl.multiple_of(p * width, 128), width)
            mine = part.at[(hop - 1) % 2, direction, :, cols]
            mine[...] = mine[...] + rs[direction, hop % 2, :, cols]
        rs_copy(direction, hop, p).start()

    def give_credit(which):
        for direction in both:
            pl.semaphore_signal(credit.at[direction, which], inc=1, device_id={'ep': origin[direction]}, device_id_type=MESH)

    def take_credit(which):
        for direction in both:
            pl.semaphore_wait(credit.at[direction, which], 1)

    def wait_sends(hop):
        with scope('wait_sends'):
            for direction in both:
                for p in (first_pieces(direction) if hop == 1 else range(pieces)):
                    rs_copy(direction, hop, p).wait_send()

    def pair(d):
        return [slot_of(1, d), slot_of(0, d)]

    points = ((0, 2), (2, 0), (3, 1))

    def gather_service(e, stage):
        for n, (at_e, at_stage) in enumerate(points):
            if stage == at_stage:
                @pl.when(e == at_e)
                def _():
                    second_step(1 + n // seconds, n % seconds)

    terms = run_experts(0, [slot_of(0, far), 0], extra=gather_service)
    steps = [(d, q) for d in range(1, far) for q in range(seconds)]
    before = (far - 2) * seconds
    with scope('combine'):
        for p in range(pieces):
            combine(0, terms[0], part.at[0, 0], p)
    for d, q in steps[len(points):before]:
        second_step(d, q)
    for j in range(pieces // 2):
        for direction in both:
            rs_copy(direction, 1, first_pieces(direction)[j]).start()
    with scope('combine'):
        for p in range(pieces):
            combine(1, terms[1], base, p)
    for d, q in steps[before:]:
        second_step(d, q)

    terms = run_experts(1, pair(far - 1))
    with scope('combine'):
        for j in range(pieces):
            for direction in both:
                p = order(direction, j)
                combine(direction, terms[direction], part.at[1, direction], p)
                forward(direction, 2, p, p in first_pieces(direction))
    give_credit(0)

    terms = run_experts(2, pair(far - 2))
    wait_sends(1)
    with scope('combine'):
        for p in range(pieces):
            for direction in both:
                combine(direction, terms[direction], part.at[0, direction], p)
    take_credit(0)

    def service(e, stage):
        if stage == 2:
            with scope('extra'):
                for direction in both:
                    forward(direction, 3, order(direction, e), True)

    terms = run_experts(3, pair(far - 3), last=True, extra=service)
    give_credit(1)
    wait_sends(2)
    with scope('combine'):
        for p in range(pieces):
            for direction in both:
                combine(direction, terms[direction], part.at[1, direction], p)

    x_all = tok[0].astype(F32) * gate_ref[...].astype(F32)
    scale = jax.nn.sigmoid(jnp.sum(x_all, axis=1, keepdims=True))

    def shared_body(i, carry):
        for which in both:
            wait_ab(which)
            up_part(lambda: tok[0], tokens, which)

            @pl.when(i == 0)
            def _():
                start_shared_ab(which, 1)
        w2_copy(0, i).wait()
        for n0, nw in chunks(hidden, 256):
            s = jnp.dot(hbuf[0:tokens, :], w2s[i, :, n0:n0 + nw], preferred_element_type=F32)
            base[:, n0:n0 + nw] = base[:, n0:n0 + nw] + scale * s
        return carry

    with scope('shared'):
        lax.fori_loop(0, 2, shared_body, 0)

    take_credit(1)
    with scope('last_hop'):
        for j in range(pieces):
            for direction in both:
                forward(direction, far, order(direction, j), True)

    with scope('finish'):
        half = pieces // 2
        for j in range(half):
            for p in (j, j + half):
                cols = pl.ds(p * width, width)
                total = tok[0, :, cols].astype(F32) + base[:, cols]
                for direction in both:
                    rs_copy(direction, far, p).wait_recv()
                    total = total + rs[direction, (far - 1) % 2, :, cols]
                out_ref[:, cols] = total.astype(BF16)

    for direction in both:
        for d in range(1, far + 1):
            for q in range(firsts):
                first_copy(direction, d, q).wait_send()
            if d < far:
                for q in range(seconds):
                    second_copy(direction, d, q).wait_send()
            if d <= meta_hops(direction):
                meta_copy(direction, d).wait_send()
    wait_sends(3)
    wait_sends(4)


def solution(mesh):
    num_ep = mesh.shape['ep']
    row_spec = P(('dp', 'ep'), None)
    replicated = P()
    expert_spec = P('ep', None, None)

    def device_step(tokens, expert_ids, gate_vals, slots, shared_w1, shared_w3, shared_w2, shared_gate, expert_w1, expert_w3, expert_w2):
        tok_count, hidden = tokens.shape
        top_k = expert_ids.shape[1]
        experts, _, ff = expert_w1.shape
        num_experts = experts * num_ep
        capacity = 8 * ((2 * tok_count * top_k + 8 * num_experts - 1) // (8 * num_experts))
        core_rows = experts * capacity
        far = num_ep // 4
        ff_a = 256 * ((ff + 511) // 512)
        ff_b = ff - ff_a

        vmem = pl.BlockSpec(memory_space=pltpu.VMEM)
        hbm = pl.BlockSpec(memory_space=pl.ANY)
        dma = pltpu.SemaphoreType.DMA
        return pl.pallas_call(
            functools.partial(moe_kernel, num_ep, capacity),
            out_shape=jax.ShapeDtypeStruct((tok_count, hidden), BF16),
            in_specs=[hbm, vmem, vmem, vmem, vmem] + [hbm] * 6,
            out_specs=vmem,
            scratch_shapes=[
                pltpu.VMEM((2 * far, tok_count, hidden), BF16),
                pltpu.VMEM((2 * far, 16, tok_count), F32),
                pltpu.VMEM((hidden, ff_a), BF16),
                pltpu.VMEM((hidden, ff_b), BF16),
                pltpu.VMEM((hidden, ff_a), BF16),
                pltpu.VMEM((hidden, ff_b), BF16),
                pltpu.VMEM((2, ff, hidden), BF16),
                pltpu.VMEM((4, core_rows, hidden), BF16),
                pltpu.VMEM((2, core_rows, hidden), BF16),
                pltpu.VMEM((4, core_rows, hidden), BF16),
                pltpu.VMEM((2, core_rows, hidden), BF16),
                pltpu.VMEM((tok_count, ff), BF16),
                pltpu.VMEM((2, 2, tok_count, hidden), F32),
                pltpu.VMEM((2, 2, tok_count, hidden), F32),
                pltpu.VMEM((tok_count, hidden), F32),
                dma((1,)), dma((2, 2)), dma((2,)),
                dma((2, far, 4)), dma((2, far, 4)), dma((2, far - 1, 2)), dma((2, far - 1, 2)), dma((2, far)), dma((2, far)),
                dma((far, 2)), dma((far, 2)), dma((far, experts)), dma((far, experts)),
                dma((2, far, 4)), dma((2, far, 4)), pltpu.SemaphoreType.REGULAR((2, 2)),
            ],
            compiler_params=pltpu.CompilerParams(collective_id=0, has_side_effects=True, vmem_limit_bytes=66_000_000),
        )(tokens, expert_ids.T, slots.T, gate_vals.T, shared_gate.reshape(1, hidden), shared_w1, shared_w3, shared_w2, expert_w1, expert_w3, expert_w2)

    return jax.shard_map(device_step, mesh=mesh, in_specs=(row_spec, row_spec, row_spec, row_spec, replicated, replicated, replicated, replicated, expert_spec, expert_spec, expert_spec), out_specs=row_spec, check_vma=False)
```

time: 274 us -> 262 us (0.956)
  Pallas kernels: 268 us -> 258 us
    pallas_call x1, Pallas kernels: 268 us -> 258 us  [device_step(): pl.pallas_call(functools.partial(moe_kernel, num_ep, capacity), out_shape...]
where the time goes in v3:
time: 262 us
  Pallas kernels  258 us (98%)
  local copies, waits for them, and re-layouts  3.59 us (1%)
    pallas_call x1, Pallas kernels, device_step(): pl.pallas_call(functools.partial(moe_kernel, num_ep, capacity), out_shape...  258 us

profile of v3, /device:TPU:21, one launch (start us, length us, event | category | flops | bytes accessed | tf_op | source)
XLA Modules:
  0.0 261.6 jit_solution(15007047511275604944)
XLA Ops:
  0.0 1.3 reshape.3.gate_ref
  1.3 258.0 %shard_map.109 = bf16[256,2048]{1,0:T(8,128)(2,1)} custom-call(bf16[256,2048]{1,0:T(8,128)(2,1)} %tok_hbm.1, s32[6,256]{1,0:T(8,128)} %bitcast.3, s32[6,256]{1,0:T(8,128)} %bitcast.4, f32[6,256]{1,0:T(8,128)} %bitcast.5, bf16[1,2048]{1,0:T(2,128)(2,1)} %reshape.3.gate_ref, bf16[2048,2816]{1,0:T(8,128)(2,1)} %ws1.1, bf16[2048,2816]{1,0:T(8,128)(2,1)} %ws3.1, ...), custom_call_target="tpu_custom_call" | custom-call | tf_op jit(solution)/shard_map/pallas_call | solution.py:454
  259.3 2.3 copy.13

commit v4 on v3

--- a/solution.py
+++ b/solution.py
@@ -19,8 +19,8 @@
 def moe_kernel(num_ep, capacity,
                tok_hbm, ids_ref, slots_ref, gates_ref, gate_ref, ws1, ws3, ws2, we1, we3, we2,
                out_ref,
-               tok, meta, w1a, w1b, w3a, w3b, w2s, xbuf, xsend, rbuf, rrecv, hbuf, part, rs, base,
-               load_sem, ab_sem, w2_sem,
+               tok, meta, w1a, w1b, w3a, w3b, w2s, xbuf, xsend, rbuf, rrecv, hbuf, part, rs, base, sels, terms, y,
+               load_sem, out_sem, ab_sem, w2_sem,
                first_send, first_recv, second_send, second_recv, meta_send, meta_recv,
                x_send, x_recv, r_send, r_recv, rs_send, rs_recv, credit):
     scope = jax.named_scope
@@ -167,19 +167,21 @@
     def position():
         return lax.broadcasted_iota(jnp.int32, (chip_rows, tokens), 0).astype(F32)
 
-    def gather(i, slot):
+    def select(i, slot):
         rel = relative(slot)
         pos = position()
         sel = jnp.zeros((chip_rows, tokens), F32)
         for k in range(top_k):
             sel = jnp.where(pos == rel[k:k + 1, :], 1.0, sel)
-        sel = sel.astype(BF16)
+        sels[i] = sel.astype(BF16)
+
+    def gather(i, slot):
         for n0, nw in chunks(hidden, 512):
-            rows = jnp.dot(sel, tok[slot, :, n0:n0 + nw], preferred_element_type=F32).astype(BF16)
+            rows = jnp.dot(sels[i], tok[slot, :, n0:n0 + nw], preferred_element_type=F32).astype(BF16)
             xbuf[i, :, n0:n0 + nw] = rows[:core_rows]
             xsend[i, :, n0:n0 + nw] = rows[core_rows:]
 
-    def weights_of(slot):
+    def weigh(i, slot):
         rel = relative(slot)
         gates = meta[slot, 8:8 + top_k, :]
         pos = position()
@@ -190,17 +192,27 @@
         hi = w.astype(BF16)
         rest = w - hi.astype(F32)
         mid = rest.astype(BF16)
-        low = (rest - mid.astype(F32)).astype(BF16)
-        return hi, mid, low
-
-    def combine(i, terms, dst, p):
+        terms[i, 0] = hi
+        terms[i, 1] = mid
+        terms[i, 2] = (rest - mid.astype(F32)).astype(BF16)
+
+    def combine(i, dst, p):
         for n0, nw in chunks(width, 256):
-            n0 = p * width + n0
-            res = jnp.concatenate([rbuf[i, :, n0:n0 + nw], rrecv[i, :, n0:n0 + nw]], axis=0)
-            acc = jnp.dot(terms[0], res, preferred_element_type=F32)
-            for term in terms[1:]:
-                acc = acc + jnp.dot(term, res, preferred_element_type=F32)
-            dst[:, n0:n0 + nw] = acc
+            cols = pl.ds(p * width + n0 if isinstance(p, int) else pl.multiple_of(p * width + n0, 128), nw)
+            res = jnp.concatenate([rbuf[i, :, cols], rrecv[i, :, cols]], axis=0)
+            acc = jnp.dot(terms[i, 0], res, preferred_element_type=F32)
+            for t in (1, 2):
+                acc = acc + jnp.dot(terms[i, t], res, preferred_element_type=F32)
+            dst[:, cols] = acc
+
+    def combine_all(*targets):
+        def body(p, carry):
+            for i, dst in targets:
+                combine(i, dst, p)
+            return carry
+
+        with scope('combine'):
+            lax.fori_loop(0, pieces, body, 0)
 
     def up_part(x_of, rows, which):
         lo, span = (0, ff_a) if which == 0 else (ff_a, ff_b)
@@ -211,8 +223,9 @@
             b = jnp.dot(x, m3[:, n0:n0 + nw], preferred_element_type=F32)
             hbuf[0:rows, lo + n0:lo + n0 + nw] = (jax.nn.silu(a) * b).astype(BF16)
 
-    def x_copy(phase, i):
-        return remote(xsend.at[i], xbuf.at[2 + i], x_send.at[phase, i], x_recv.at[phase, i], partner)
+    def x_copy(phase, i, e):
+        rows = pl.ds(pl.multiple_of(e * capacity, 16), capacity)
+        return remote(xsend.at[i, rows], xbuf.at[2 + i, rows], x_send.at[phase, i, e], x_recv.at[phase, i, e], partner)
 
     def r_copy(phase, e):
         rows = pl.ds(pl.multiple_of(e * capacity, 16), capacity)
@@ -222,6 +235,14 @@
         def body(e, carry):
             row0 = pl.multiple_of(e * capacity, 16)
             nxt = (e + 1) % experts
+            with scope('x_wait'):
+                for i in both:
+                    x_copy(phase, i, e).wait_recv()
+
+            @pl.when(e < experts - 1)
+            def _():
+                for i in both:
+                    x_copy(phase, i, e + 1).start()
 
             def x_of():
                 return jnp.concatenate([xbuf[s, pl.ds(row0, capacity), :] for s in range(4)], axis=0)
@@ -243,6 +264,18 @@
                     start_ab(which, nxt)
                 if extra is not None:
                     extra(e, which)
+            if last:
+                @pl.when((e >= 1) & (e < experts - 1))
+                def _():
+                    w2_copy(nxt, nxt % 2).start()
+
+                @pl.when(e == experts - 1)
+                def _():
+                    shared_w2_copy(0, 0).start()
+            else:
+                @pl.when(e >= 1)
+                def _():
+                    w2_copy(nxt, nxt % 2).start()
             slot = e % 2
             with scope('wait_w2'):
                 w2_copy(0, slot).wait()
@@ -252,17 +285,14 @@
                     for s in range(4):
                         rbuf[s, pl.ds(row0, capacity), n0:n0 + nw] = r[s * capacity:(s + 1) * capacity]
             r_copy(phase, e).start()
-            if last:
-                @pl.when(e < experts - 2)
-                def _():
-                    w2_copy(e + 2, slot).start()
-
-                for i in both:
-                    @pl.when(e == experts - 2 + i)
-                    def _():
-                        shared_w2_copy(i, i).start()
-            else:
-                w2_copy((e + 2) % experts, slot).start()
+
+            @pl.when(e == experts - 1)
+            def _():
+                if last:
+                    shared_w2_copy(1, 1).start()
+                else:
+                    w2_copy(1, 1).start()
+
             if extra is not None:
                 extra(e, 2)
             return carry
@@ -270,21 +300,23 @@
         with scope('experts'):
             lax.fori_loop(0, experts, body, 0)
 
-    def run_experts(phase, slots, last=False, extra=None):
+    def run_experts(phase, slots, last=False, extra=None, prepared=False):
         with scope('gather'):
             for i in both:
+                if not prepared:
+                    select(i, slots[i])
                 gather(i, slots[i])
-                x_copy(phase, i).start()
-        with scope('x_swap'):
+                x_copy(phase, i, 0).start()
+        expert_loop(phase, last, extra)
+        with scope('weigh'):
             for i in both:
-                x_copy(phase, i).wait()
-        expert_loop(phase, last, extra)
-        with scope('weights'):
-            terms = [weights_of(slot) for slot in slots]
+                if not prepared:
+                    weigh(i, slots[i])
         with scope('r_swap'):
             for e in range(experts):
+                for i in both:
+                    x_copy(phase, i, e).wait_send()
                 r_copy(phase, e).wait()
-        return terms
 
     def rs_copy(direction, hop, p):
         cols = pl.ds(p * width if isinstance(p, int) else pl.multiple_of(p * width, 128), width)
@@ -324,7 +356,7 @@
     def pair(d):
         return [slot_of(1, d), slot_of(0, d)]
 
-    points = ((0, 2), (2, 0), (3, 1))
+    points = ((1, 0), (2, 1), (3, 2))
 
     def gather_service(e, stage):
         for n, (at_e, at_stage) in enumerate(points):
@@ -333,38 +365,34 @@
                 def _():
                     second_step(1 + n // seconds, n % seconds)
 
-    terms = run_experts(0, [slot_of(0, far), 0], extra=gather_service)
+    run_experts(0, [slot_of(0, far), 0], extra=gather_service)
     steps = [(d, q) for d in range(1, far) for q in range(seconds)]
     before = (far - 2) * seconds
-    with scope('combine'):
-        for p in range(pieces):
-            combine(0, terms[0], part.at[0, 0], p)
+    combine_all((0, part.at[0, 0]))
     for d, q in steps[len(points):before]:
         second_step(d, q)
     for j in range(pieces // 2):
         for direction in both:
             rs_copy(direction, 1, first_pieces(direction)[j]).start()
-    with scope('combine'):
-        for p in range(pieces):
-            combine(1, terms[1], base, p)
+    combine_all((1, base))
+    for i in both:
+        select(i, pair(far - 1)[i])
+        weigh(i, pair(far - 1)[i])
     for d, q in steps[before:]:
         second_step(d, q)
 
-    terms = run_experts(1, pair(far - 1))
+    run_experts(1, pair(far - 1), prepared=True)
     with scope('combine'):
         for j in range(pieces):
             for direction in both:
                 p = order(direction, j)
-                combine(direction, terms[direction], part.at[1, direction], p)
+                combine(direction, part.at[1, direction], p)
                 forward(direction, 2, p, p in first_pieces(direction))
     give_credit(0)
 
-    terms = run_experts(2, pair(far - 2))
+    run_experts(2, pair(far - 2))
     wait_sends(1)
-    with scope('combine'):
-        for p in range(pieces):
-            for direction in both:
-                combine(direction, terms[direction], part.at[0, direction], p)
+    combine_all((0, part.at[0, 0]), (1, part.at[0, 1]))
     take_credit(0)
 
     def service(e, stage):
@@ -373,16 +401,15 @@
                 for direction in both:
                     forward(direction, 3, order(direction, e), True)
 
-    terms = run_experts(3, pair(far - 3), last=True, extra=service)
+    run_experts(3, pair(far - 3), last=True, extra=service)
     give_credit(1)
     wait_sends(2)
-    with scope('combine'):
-        for p in range(pieces):
-            for direction in both:
-                combine(direction, terms[direction], part.at[1, direction], p)
-
-    x_all = tok[0].astype(F32) * gate_ref[...].astype(F32)
-    scale = jax.nn.sigmoid(jnp.sum(x_all, axis=1, keepdims=True))
+    combine_all((0, part.at[1, 0]), (1, part.at[1, 1]))
+
+    products = jnp.zeros((tokens, 128), F32)
+    for j in range(hidden // 128):
+        products = products + tok[0, :, j * 128:(j + 1) * 128].astype(F32) * gate_ref[j:j + 1, :].astype(F32)
+    scale = jax.nn.sigmoid(jnp.sum(products, axis=1, keepdims=True))
 
     def shared_body(i, carry):
         for which in both:
@@ -416,7 +443,8 @@
                 for direction in both:
                     rs_copy(direction, far, p).wait_recv()
                     total = total + rs[direction, (far - 1) % 2, :, cols]
-                out_ref[:, cols] = total.astype(BF16)
+                y[:, cols] = total.astype(BF16)
+                pltpu.make_async_copy(y.at[:, cols], out_ref.at[:, cols], out_sem.at[p]).start()
 
     for direction in both:
         for d in range(1, far + 1):
@@ -429,6 +457,10 @@
                 meta_copy(direction, d).wait_send()
     wait_sends(3)
     wait_sends(4)
+    with scope('out'):
+        for p in range(pieces):
+            cols = pl.ds(p * width, width)
+            pltpu.make_async_copy(y.at[:, cols], out_ref.at[:, cols], out_sem.at[p]).wait()
 
 
 def solution(mesh):
@@ -455,7 +487,7 @@
             functools.partial(moe_kernel, num_ep, capacity),
             out_shape=jax.ShapeDtypeStruct((tok_count, hidden), BF16),
             in_specs=[hbm, vmem, vmem, vmem, vmem] + [hbm] * 6,
-            out_specs=vmem,
+            out_specs=hbm,
             scratch_shapes=[
                 pltpu.VMEM((2 * far, tok_count, hidden), BF16),
                 pltpu.VMEM((2 * far, 16, tok_count), F32),
@@ -472,12 +504,15 @@
                 pltpu.VMEM((2, 2, tok_count, hidden), F32),
                 pltpu.VMEM((2, 2, tok_count, hidden), F32),
                 pltpu.VMEM((tok_count, hidden), F32),
-                dma((1,)), dma((2, 2)), dma((2,)),
+                pltpu.VMEM((2, 2 * core_rows, tok_count), BF16),
+                pltpu.VMEM((2, 3, tok_count, 2 * core_rows), BF16),
+                pltpu.VMEM((tok_count, hidden), BF16),
+                dma((1,)), dma((4,)), dma((2, 2)), dma((2,)),
                 dma((2, far, 4)), dma((2, far, 4)), dma((2, far - 1, 2)), dma((2, far - 1, 2)), dma((2, far)), dma((2, far)),
-                dma((far, 2)), dma((far, 2)), dma((far, experts)), dma((far, experts)),
+                dma((far, 2, experts)), dma((far, 2, experts)), dma((far, experts)), dma((far, experts)),
                 dma((2, far, 4)), dma((2, far, 4)), pltpu.SemaphoreType.REGULAR((2, 2)),
             ],
             compiler_params=pltpu.CompilerParams(collective_id=0, has_side_effects=True, vmem_limit_bytes=66_000_000),
-        )(tokens, expert_ids.T, slots.T, gate_vals.T, shared_gate.reshape(1, hidden), shared_w1, shared_w3, shared_w2, expert_w1, expert_w3, expert_w2)
+        )(tokens, expert_ids.T, slots.T, gate_vals.T, shared_gate.reshape(hidden // 128, 128), shared_w1, shared_w3, shared_w2, expert_w1, expert_w3, expert_w2)
 
     return jax.shard_map(device_step, mesh=mesh, in_specs=(row_spec, row_spec, row_spec, row_spec, replicated, replicated, replicated, replicated, expert_spec, expert_spec, expert_spec), out_specs=row_spec, check_vma=False)

time: 262 us -> 258 us (0.985)
  no operation moved by 1% of the time
where the time goes in v4:
time: 258 us
  Pallas kernels  256 us (99%)
    pallas_call x1, Pallas kernels, device_step(): pl.pallas_call(functools.partial(moe_kernel, num_ep, capacity), out_shape...  256 us

profile of v4, /device:TPU:21, one launch (start us, length us, event | category | flops | bytes accessed | tf_op | source)
XLA Modules:
  0.0 258.0 jit_solution(9195829126007441013)
XLA Ops:
  0.0 255.7 %shard_map.109 = bf16[256,2048]{1,0:T(8,128)(2,1)} custom-call(bf16[256,2048]{1,0:T(8,128)(2,1)} %tok_hbm.1, s32[6,256]{1,0:T(8,128)} %bitcast.4, s32[6,256]{1,0:T(8,128)} %bitcast.5, f32[6,256]{1,0:T(8,128)} %bitcast.6, bf16[16,128]{1,0:T(8,128)(2,1)} %bitcast.7, bf16[2048,2816]{1,0:T(8,128)(2,1)} %ws1.1, bf16[2048,2816]{1,0:T(8,128)(2,1)} %ws3.1, ...), custom_call_target="tpu_custom_call" | custom-call | tf_op jit(solution)/shard_map/pallas_call | solution.py:486
  255.7 2.3 copy.13

commit v5 on v4

--- a/solution.py
+++ b/solution.py
@@ -223,13 +223,13 @@
             b = jnp.dot(x, m3[:, n0:n0 + nw], preferred_element_type=F32)
             hbuf[0:rows, lo + n0:lo + n0 + nw] = (jax.nn.silu(a) * b).astype(BF16)
 
-    def x_copy(phase, i, e):
+    def x_copy(i, e):
         rows = pl.ds(pl.multiple_of(e * capacity, 16), capacity)
-        return remote(xsend.at[i, rows], xbuf.at[2 + i, rows], x_send.at[phase, i, e], x_recv.at[phase, i, e], partner)
-
-    def r_copy(phase, e):
+        return remote(xsend.at[i, rows], xbuf.at[2 + i, rows], x_send.at[i, e], x_recv.at[i, e], partner)
+
+    def r_copy(e):
         rows = pl.ds(pl.multiple_of(e * capacity, 16), capacity)
-        return remote(rbuf.at[pl.ds(2, 2), rows], rrecv.at[:, rows], r_send.at[phase, e], r_recv.at[phase, e], partner)
+        return remote(rbuf.at[pl.ds(2, 2), rows], rrecv.at[:, rows], r_send.at[e], r_recv.at[e], partner)
 
     def expert_loop(phase, last, extra):
         def body(e, carry):
@@ -237,12 +237,12 @@
             nxt = (e + 1) % experts
             with scope('x_wait'):
                 for i in both:
-                    x_copy(phase, i, e).wait_recv()
+                    x_copy(i, e).wait_recv()
 
             @pl.when(e < experts - 1)
             def _():
                 for i in both:
-                    x_copy(phase, i, e + 1).start()
+                    x_copy(i, e + 1).start()
 
             def x_of():
                 return jnp.concatenate([xbuf[s, pl.ds(row0, capacity), :] for s in range(4)], axis=0)
@@ -284,7 +284,7 @@
                     r = jnp.dot(hbuf[0:4 * capacity, :], w2s[slot, :, n0:n0 + nw], preferred_element_type=F32).astype(BF16)
                     for s in range(4):
                         rbuf[s, pl.ds(row0, capacity), n0:n0 + nw] = r[s * capacity:(s + 1) * capacity]
-            r_copy(phase, e).start()
+            r_copy(e).start()
 
             @pl.when(e == experts - 1)
             def _():
@@ -306,7 +306,7 @@
                 if not prepared:
                     select(i, slots[i])
                 gather(i, slots[i])
-                x_copy(phase, i, 0).start()
+                x_copy(i, 0).start()
         expert_loop(phase, last, extra)
         with scope('weigh'):
             for i in both:
@@ -315,14 +315,14 @@
         with scope('r_swap'):
             for e in range(experts):
                 for i in both:
-                    x_copy(phase, i, e).wait_send()
-                r_copy(phase, e).wait()
+                    x_copy(i, e).wait_send()
+                r_copy(e).wait()
 
     def rs_copy(direction, hop, p):
         cols = pl.ds(p * width if isinstance(p, int) else pl.multiple_of(p * width, 128), width)
         src = part.at[0, 0, :, cols] if hop == 1 else part.at[(hop - 1) % 2, direction, :, cols]
         return remote(src, rs.at[direction, (hop - 1) % 2, :, cols],
-                      rs_send.at[direction, hop - 1, p], rs_recv.at[direction, hop - 1, p], towards[direction])
+                      rs_send.at[direction, (hop - 1) % 2, p], rs_recv.at[direction, (hop - 1) % 2, p], towards[direction])
 
     def first_pieces(direction):
         half = pieces // 2
@@ -509,8 +509,8 @@
                 pltpu.VMEM((tok_count, hidden), BF16),
                 dma((1,)), dma((4,)), dma((2, 2)), dma((2,)),
                 dma((2, far, 4)), dma((2, far, 4)), dma((2, far - 1, 2)), dma((2, far - 1, 2)), dma((2, far)), dma((2, far)),
-                dma((far, 2, experts)), dma((far, 2, experts)), dma((far, experts)), dma((far, experts)),
-                dma((2, far, 4)), dma((2, far, 4)), pltpu.SemaphoreType.REGULAR((2, 2)),
+                dma((2, experts)), dma((2, experts)), dma((experts,)), dma((experts,)),
+                dma((2, 2, 4)), dma((2, 2, 4)), pltpu.SemaphoreType.REGULAR((2, 2)),
             ],
             compiler_params=pltpu.CompilerParams(collective_id=0, has_side_effects=True, vmem_limit_bytes=66_000_000),
         )(tokens, expert_ids.T, slots.T, gate_vals.T, shared_gate.reshape(hidden // 128, 128), shared_w1, shared_w3, shared_w2, expert_w1, expert_w3, expert_w2)

time: 258 us -> 257 us (level)
  no operation moved by 1% of the time
where the time goes in v5:
time: 257 us
  Pallas kernels  255 us (99%)
    pallas_call x1, Pallas kernels, device_step(): pl.pallas_call(functools.partial(moe_kernel, num_ep, capacity), out_shape...  255 us

profile of v5, /device:TPU:21, one launch (start us, length us, event | category | flops | bytes accessed | tf_op | source)
XLA Modules:
  0.0 257.1 jit_solution(9649867414554013982)
XLA Ops:
  0.0 254.8 %shard_map.109 = bf16[256,2048]{1,0:T(8,128)(2,1)} custom-call(bf16[256,2048]{1,0:T(8,128)(2,1)} %tok_hbm.1, s32[6,256]{1,0:T(8,128)} %bitcast.4, s32[6,256]{1,0:T(8,128)} %bitcast.5, f32[6,256]{1,0:T(8,128)} %bitcast.6, bf16[16,128]{1,0:T(8,128)(2,1)} %bitcast.7, bf16[2048,2816]{1,0:T(8,128)(2,1)} %ws1.1, bf16[2048,2816]{1,0:T(8,128)(2,1)} %ws3.1, ...), custom_call_target="tpu_custom_call" | custom-call | tf_op jit(solution)/shard_map/pallas_call | solution.py:486
  254.8 2.3 copy.13
